TPU v7x, 32 devices: a 4x4x1 block of a 4x4x8 slice. The times are simulated.
32 devices in a mesh: data: 1 (over z), seq: 32 (over y, x, core).
Axes of the slice: x: 4, y: 4, z: 1, core: 2. Of those that a mesh axis runs over, the one named last changes fastest.
The devices are a block of a 4x4x8 slice.
Arguments:
- tokens: bfloat16 [16, 4096, 768], P('data', 'seq')
- lengths: int32 [16], P('data')
- slot_params: bfloat16 [768, 128], replicated
- logit_scale: float32 [1], replicated
- w_in: bfloat16 [128, 768, 3072], P('seq')
- w_out: bfloat16 [128, 3072, 768], P('seq')
Outputs:
- output: bfloat16 [16, 4096, 768], P('data', 'seq')
All inputs are finite; a program needn't handle non-finite values.
Results may differ from a plain program's by a relative error of at most 0.0156646.
Values are sent between devices in bfloat16 or wider.
A program may use at most 768 MiB of HBM per device.

v0:
```python
import jax
import jax.numpy as jnp
from jax import lax
from jax.sharding import PartitionSpec as P


def solution(mesh):
    seq_size = mesh.shape["seq"]

    def shard_body(tok_blk, len_blk, slot_params, logit_scale, w_in_blk, w_out_blk):
        num_rows, tok_count, model_width = tok_blk.shape
        num_slots = slot_params.shape[1]
        own_slots = num_slots // seq_size
        local_experts = w_in_blk.shape[0]
        slots_per = own_slots // local_experts
        shard_idx = lax.axis_index("seq")
        params_f32 = slot_params.astype(jnp.float32)
        col_inv = lax.rsqrt(jnp.sum(params_f32 * params_f32, axis=0, keepdims=True) + 1e-6)
        phi_norm = (params_f32 * (logit_scale[0] * col_inv)).astype(jnp.bfloat16)
        tok_f32 = tok_blk.astype(jnp.float32)
        tok_norm = (tok_f32 * lax.rsqrt(jnp.sum(tok_f32 * tok_f32, axis=-1, keepdims=True) + 1e-6)).astype(jnp.bfloat16)
        logits = jnp.einsum("btd,dn->btn", tok_norm, phi_norm, preferred_element_type=jnp.float32)
        positions = shard_idx * tok_count + jnp.arange(tok_count)
        is_valid = (positions[None, :] < len_blk[:, None])[:, :, None]
        local_max = jnp.max(jnp.where(is_valid, logits, -jnp.inf), axis=1)
        col_max = lax.pmax(local_max, "seq")
        disp_w = jnp.where(is_valid, jnp.exp(logits - col_max[:, None, :]), 0.0)
        col_sum = lax.psum(jnp.sum(disp_w, axis=1), "seq")
        part_sum = jnp.einsum("btn,btd->bnd", disp_w.astype(jnp.bfloat16), tok_blk, preferred_element_type=jnp.float32).astype(jnp.bfloat16)
        slot_sum = lax.psum_scatter(part_sum, "seq", scatter_dimension=1, tiled=True)
        own_sum = lax.dynamic_slice_in_dim(col_sum, shard_idx * own_slots, own_slots, axis=1)
        slot_in = (slot_sum.astype(jnp.float32) / own_sum[:, :, None]).astype(jnp.bfloat16)
        slot_in = slot_in.reshape(num_rows, local_experts, slots_per, model_width)
        hidden = jax.nn.gelu(jnp.einsum("besd,edf->besf", slot_in, w_in_blk, preferred_element_type=jnp.float32)).astype(jnp.bfloat16)
        slot_out = jnp.einsum("besf,efd->besd", hidden, w_out_blk, preferred_element_type=jnp.float32).astype(jnp.bfloat16)
        slot_out = slot_out.reshape(num_rows, own_slots, model_width)
        all_out = lax.all_gather(slot_out, "seq", axis=1, tiled=True)
        combine_w = jax.nn.softmax(logits, axis=-1).astype(jnp.bfloat16)
        mixed = jnp.einsum("btn,bnd->btd", combine_w, all_out, preferred_element_type=jnp.float32).astype(jnp.bfloat16)
        return jnp.where(is_valid, mixed, jnp.zeros_like(mixed))

    return jax.shard_map(
        shard_body,
        mesh=mesh,
        in_specs=(P("data", "seq", None), P("data"), P(None, None), P(None), P("seq", None, None), P("seq", None, None)),
        out_specs=P("data", "seq", None),
        check_vma=False,
    )
```

profile of v0, /device:TPU:97, one launch (start us, length us, event | category | flops | bytes accessed | tf_op | source)
XLA Modules:
  0.0 209.7 jit_solution(9392756411842081961)
XLA Ops:
  6.5 0.0 copy-start
  6.5 0.0 copy-start.2
  6.6 0.0 copy-start.3
  6.6 0.0 reduce-scatter.2.cloned.1.call-start
  6.6 2.7 %fusion.1 = f32[16,128]{1,0:T(8,128)S(1)} fusion(bf16[16,128,768]{2,1,0:T(8,128)(2,1)} %param.6), kind=kLoop, calls=%fused_computation.3 | loop fusion | flops 4716544 | bytes 3153920 | tf_op jit(solution)/shard_map/reduce_sum | solution.py:21
  10.0 1.0 fusion.31
  11.0 0.0 copy-done.3
  11.0 0.1 broadcast_compare_fusion
  11.1 0.0 copy-done
  11.1 0.0 copy-done.2
  11.1 2.1 %select_reduce_fusion = (f32[16,128]{1,0:T(8,128)S(1)}, f32[16,128,128]{2,1,0:T(8,128)}) fusion(pred[16,128]{1,0:T(8,128)(4,1)S(1)} %broadcast_compare_fusion, bf16[768,128]{1,0:T(8,128)(2,1)S(1)} %copy-done.2, f32[128]{0:T(128)S(1)} %rsqrt_multiply_fusion, bf16[16,128,768]{2,1,0:T(8,128)(2,1)S(1)} %copy-done, f32[16,128]{1,0:T(8,128)S(1)} %add_rsqrt_fusion), kind=kOutput, calls=%fused_computation.19 | convolution fusion | flops 408188928 | bytes 4409856 | tf_op jit(solution)/shard_map/btd,dn->btn/dot_general | solution.py:22
  13.2 49.8 %pmax.7 = f32[16,128]{1,0:T(8,128)S(1)} all-reduce(f32[16,128]{1,0:T(8,128)S(1)} %get-tuple-element.5), channel_id=1, replica_groups=mesh['data'=1,'seq'=32] {'seq'}, use_global_device_ids=true, to_apply=%region_5.6 | all-reduce | flops 2048 | bytes 16384 | tf_op jit(solution)/shard_map/pmax | solution.py:26
  63.0 2.8 %fusion.25 = bf16[16,128,768]{2,1,0:T(8,128)(2,1)S(1)} fusion(bf16[16,128,768]{2,1,0:T(8,128)(2,1)S(1)} %copy-done, f32[16,128,128]{2,1,0:T(8,128)} %get-tuple-element.6, f32[16,128]{1,0:T(8,128)S(1)} %pmax.7, pred[16,128]{1,0:T(8,128)(4,1)S(1)} %broadcast_compare_fusion), kind=kOutput, calls=%fused_computation.32 | convolution fusion | flops 403439616 | bytes 7350272 | tf_op jit(solution)/shard_map/btn,btd->bnd/dot_general | solution.py:29
  65.7 3.4 %copy.19 = bf16[16,128,768]{2,0,1:T(8,128)(2,1)} copy(bf16[16,128,768]{2,1,0:T(8,128)(2,1)S(1)} %fusion.25) | data formatting | bytes 6291456 | tf_op jit(solution)/shard_map/btn,btd->bnd/dot_general | solution.py:29
  69.2 0.0 copy-start.1
  69.2 0.1 reduce-scatter.2.cloned.1.call-update
  69.2 0.1 all-gather.3.cloned.1.call-start
  69.3 1.1 copy-done.1
  70.4 0.4 fusion.14
  70.8 44.1 %psum.7 = f32[16,128]{1,0:T(8,128)S(1)} all-reduce(f32[16,128]{1,0:T(8,128)S(1)} %fusion.14), channel_id=1, replica_groups=mesh['data'=1,'seq'=32] {'seq'}, use_global_device_ids=true, to_apply=%region_8.9 | all-reduce | flops 2048 | bytes 16384 | tf_op jit(solution)/shard_map/psum | solution.py:28
  114.9 0.1 constant_dynamic-slice_fusion
  115.0 0.1 copy.8
  115.0 23.8 %reduce-scatter.2.cloned.1.call-done = bf16[16,4,768]{2,0,1:T(8,128)(2,1)} async-done(((bf16[16,128,768]{2,0,1:T(8,128)(2,1)}), bf16[16,4,768]{2,0,1:T(8,128)(2,1)}) %reduce-scatter.2.cloned.1.call-update) | async-done | bytes 98320 | tf_op jit(solution)/shard_map/reduce_scatter | solution.py:30
  138.8 15.0 %fusion.13 = bf16[16,4,1,768]{3,0,2,1:T(8,128)(2,1)} fusion(bf16[4,3072,768]{2,1,0:T(8,128)(2,1)} %param.11, bf16[4,768,3072]{2,1,0:T(8,128)(2,1)} %param.10, bf16[16,4,768]{2,0,1:T(8,128)(2,1)} %reduce-scatter.2.cloned.1.call-done, f32[16,4]{0,1:T(4,128)S(1)} %copy.8), kind=kOutput, calls=%fused_computation.17 | convolution fusion | flops 605945856 | bytes 37945600 | tf_op jit(solution)/shard_map/besf,efd->besd/dot_general | solution.py:35
  153.8 0.1 all-gather.3.cloned.1.call-update
  153.9 0.6 fusion.48
  154.5 40.6 %all-gather.3.cloned.1.call-done = bf16[16,128,1,768]{3,0,2,1:T(8,128)(2,1)} async-done(((bf16[16,4,1,768]{3,0,2,1:T(8,128)(2,1)}), bf16[16,128,1,768]{3,0,2,1:T(8,128)(2,1)}) %all-gather.3.cloned.1.call-update) | async-done | bytes 3145744 | tf_op jit(solution)/shard_map/all_gather | solution.py:37
  195.1 7.7 %convert_select_fusion = bf16[16,128,768]{2,1,0:T(8,128)(2,1)} fusion(pred[16,128]{1,0:T(8,128)(4,1)S(1)} %broadcast_compare_fusion, bf16[16,128,1,768]{3,0,2,1:T(8,128)(2,1)} %all-gather.3.cloned.1.call-done, f32[16,128]{1,0:T(8,128)S(1)} %fusion.48, f32[16,128,128]{2,1,0:T(8,128)S(1)} %copy-done.1), kind=kOutput, calls=%fused_computation.11 | convolution fusion | flops 406587520 | bytes 7350272 | tf_op jit(solution)/shard_map/btn,bnd->btd/dot_general | solution.py:39
  (3 shorter events, 0.0 us)
Async XLA Ops:
  6.5 4.5 %copy-start = (bf16[16,128,768]{2,1,0:T(8,128)(2,1)S(1)}, bf16[16,128,768]{2,1,0:T(8,128)(2,1)}, u32[]{:S(2)}) copy-start(bf16[16,128,768]{2,1,0:T(8,128)(2,1)} %param.6) | copy-start | bytes 9437188
  6.5 4.5 %copy-start.2 = (bf16[768,128]{1,0:T(8,128)(2,1)S(1)}, bf16[768,128]{1,0:T(8,128)(2,1)}, u32[]{:S(2)}) copy-start(bf16[768,128]{1,0:T(8,128)(2,1)} %param.8) | copy-start | bytes 589828
  6.6 4.5 %copy-start.3 = (s32[16]{0:T(128)S(1)}, s32[16]{0:T(128)}, u32[]{:S(2)}) copy-start(s32[16]{0:T(128)} %param.7) | copy-start | bytes 196
  6.6 132.2 %reduce-scatter.2.cloned.1.call-start = ((), (), s32[]{:S(2)}) async-start(), calls=%async_computation.1 | async-start | bytes 3244032 | tf_op jit(solution)/shard_map/reduce_scatter | solution.py:30
  69.2 1.2 copy-start.1
  69.2 125.9 %all-gather.3.cloned.1.call-start = ((), (), s32[]{:S(2)}) async-start(), calls=%async_computation.2 | async-start | bytes 3244032 | tf_op jit(solution)/shard_map/all_gather | solution.py:37
Sparse Core Ops, SparseCore 0:
  69.3 69.4 reduce-scatter.1
  154.0 41.0 all-gather.2
where the time goes:
time: 210 us
  blocking collectives  93.9 us (45%)
  waiting for transfers between devices  64.5 us (31%)
  matrix products  27.6 us (13%)
  between operations  14.1 us (7%)
  other arithmetic  4.88 us (2%)
  local copies, waits for them, and re-layouts  4.66 us (2%)
    pmax x1, blocking collectives, shard_body(): col_max = lax.pmax(local_max, 'seq')  49.8 us
    psum x1, blocking collectives, shard_body(): col_sum = lax.psum(jnp.sum(disp_w, axis=1), 'seq')  44.1 us
    all_gather x1, waiting for transfers between devices, shard_body(): all_out = lax.all_gather(slot_out, 'seq', axis=1, tiled=True)  40.6 us
    reduce_scatter x1, waiting for transfers between devices, shard_body(): lax.psum_scatter(part_sum, 'seq', scatter_dimension=1, tiled=True)  23.8 us
    dot_general x1, matrix products, shard_body(): jnp.einsum('besf,efd->besd', hidden, w_out_blk, preferred_element_type=jn...  15 us
    dot_general x1, matrix products, shard_body(): jnp.einsum('btn,bnd->btd', combine_w, all_out, preferred_element_type=jnp...  7.7 us
  transfers between devices with their start and end apart: 2, of which 2 were waited for; matrix products, arithmetic and copies ran while one was open for 1% of the time, Pallas kernels for 0%

commit v1 on v0

v1 whole, which is shorter than its diff:
```python
import functools

import jax
import jax.numpy as jnp
from jax import lax
from jax.experimental import pallas as pl
from jax.experimental.pallas import tpu as pltpu
from jax.sharding import PartitionSpec as P

CHUNK = 256
NDIM = 4
F32 = jnp.float32
BF16 = jnp.bfloat16
MESH = pl.DeviceIdType.MESH


def _nt(a, b):
    return lax.dot_general(a, b, (((1,), (1,)), ((), ())), preferred_element_type=F32)


def _nn(a, b):
    return jnp.dot(a, b, preferred_element_type=F32)


def _kernel(len_ref, gain_ref, tok_hbm, phi_hbm, wi_hbm, wo_hbm, y_hbm,
            x_v, phi_v, phit_v, wi_v, wo_v, ct_v, c_v, part, half_in, r0, r1, r2, r3,
            z_part, z_half, z0, z1, z2, z3, xs, xs_f, hid, hid_b, ys_f, yx, yx_in, gath,
            tok_sem, phi_sem, wi_sem, wo_sem, out_sem,
            hs_sem, hr_sem, zhs_sem, zhr_sem, zs_sem, zr_sem, rs_sem, rr_sem,
            xss_sem, xsr_sem, yxs_sem, yxr_sem, gs_sem, gr_sem, gds_sem, gdr_sem):
    rows, tok_count, width = x_v.shape
    experts = wi_v.shape[0]
    nk = width // CHUNK
    hrows = rows // 2
    gsz = hrows // NDIM
    nslots = phit_v.shape[0]
    chip_rows = 2 * experts
    me = lax.axis_index("seq")
    core = lax.rem(me, 2)
    chip = me // 2
    x = lax.rem(chip, 4)
    y = chip // 4
    xb = x // 2
    xa = lax.rem(x + xb, 2)
    yb = y // 2
    ya = lax.rem(y + yb, 2)
    bits = (yb, ya, xb, xa)

    def dev(yy, xx, cc):
        return {"seq": (yy * 4 + xx) * 2 + cc}

    mate = dev(y, x, 1 - core)
    flips = (
        dev(3 - y, x, core),
        dev(y + 1 - 2 * lax.rem(y, 2), x, core),
        dev(y, 3 - x, core),
        dev(y, x + 1 - 2 * lax.rem(x, 2), core),
    )
    orders = ((3, 1, 2, 0), (1, 2, 0, 3), (2, 0, 3, 1), (0, 3, 1, 2))
    own0 = core * hrows
    oth0 = (1 - core) * hrows

    barrier = pltpu.get_barrier_semaphore()
    for d in flips + (mate,):
        pl.semaphore_signal(barrier, inc=1, device_id=d, device_id_type=MESH)

    def tok_copy(b):
        return pltpu.make_async_copy(tok_hbm.at[b], x_v.at[b], tok_sem.at[b])

    phi_copy = pltpu.make_async_copy(phi_hbm, phi_v, phi_sem)
    phi_copy.start()
    for j in range(rows):
        tok_copy(lax.rem(oth0 + j, rows)).start()
    wi_copies = [pltpu.make_async_copy(wi_hbm.at[e], wi_v.at[e], wi_sem.at[e]) for e in range(experts)]
    wo_copies = [pltpu.make_async_copy(wo_hbm.at[e], wo_v.at[e], wo_sem.at[e]) for e in range(experts)]

    z_part[...] = jnp.zeros_like(z_part)
    ys_f[...] = jnp.zeros_like(ys_f)

    gain = gain_ref[0]
    shift = gain * (1.0 + 2.0 ** -7)
    phi_copy.wait()
    pf = phi_v[...].astype(F32)
    pn = (pf * (gain * lax.rsqrt(jnp.sum(pf * pf, axis=0, keepdims=True) + 1e-6))).astype(BF16)
    new = lax.broadcasted_iota(jnp.int32, (nslots, nslots), 0)
    old = lax.broadcasted_iota(jnp.int32, (nslots, nslots), 1)
    nchip = new // chip_rows
    nxa, nxb, nya, nyb = nchip & 1, (nchip >> 1) & 1, (nchip >> 2) & 1, (nchip >> 3) & 1
    src = ((2 * nyb + (nya ^ nyb)) * 4 + 2 * nxb + (nxa ^ nxb)) * chip_rows + (new & (chip_rows - 1))
    perm = jnp.where(src == old, 1.0, 0.0).astype(BF16)
    phit_v[...] = _nt(perm, pn).astype(BF16)

    lane = lax.broadcasted_iota(jnp.int32, (nslots, tok_count), 1)
    pos = me * tok_count + lane

    def front(b0):
        zs = []
        for u in range(gsz):
            b = b0 + u
            tok_copy(b).wait()
            xv = x_v[b]
            xf = xv.astype(F32)
            xn = (xf * lax.rsqrt(jnp.sum(xf * xf, axis=1, keepdims=True) + 1e-6)).astype(BF16)
            ex = jnp.exp(_nt(phit_v[...], xn) - shift)
            ct_v[b] = (ex * (1.0 / jnp.sum(ex, axis=0, keepdims=True))).astype(BF16)
            exm = jnp.where(pos < len_ref[b], ex, 0.0)
            zs.append(jnp.where(lane == b, jnp.sum(exm, axis=1, keepdims=True), 0.0))
            w = exm.astype(BF16)
            for k in range(nk):
                pk = _nn(w, xv[:, k * CHUNK:(k + 1) * CHUNK])
                part[k, b] = pk.reshape(2, 2, 2, 2, chip_rows, CHUNK).astype(BF16)
        z_part[...] += functools.reduce(jnp.add, zs).reshape(z_part.shape)

    def half_copy(q):
        return pltpu.make_async_remote_copy(
            part.at[:, pl.ds(oth0 + q * gsz, gsz)], half_in.at[:, pl.ds(q * gsz, gsz)],
            hs_sem.at[q], hr_sem.at[q], device_id=mate, device_id_type=MESH)

    def where_(order, s, flip):
        idx = [slice(None)] * NDIM
        for t in range(s):
            idx[order[t]] = bits[order[t]]
        if flip:
            idx[order[s]] = 1 - bits[order[s]]
        return tuple(idx)

    rbuf = (r0, r1, r2, r3)
    zbuf = (z0, z1, z2, z3)

    def rs_copy(k, q, s):
        order = orders[q]
        i = (k * NDIM + q) * NDIM + s
        return pltpu.make_async_remote_copy(
            part.at[(k, pl.ds(own0 + q * gsz, gsz)) + where_(order, s, True)],
            rbuf[s].at[k, pl.ds(q * gsz, gsz)],
            rs_sem.at[i], rr_sem.at[i], device_id=flips[order[s]], device_id_type=MESH)

    def z_copy(s):
        order = orders[0]
        return pltpu.make_async_remote_copy(
            z_part.at[where_(order, s, True)], zbuf[s],
            zs_sem.at[s], zr_sem.at[s], device_id=flips[order[s]], device_id_type=MESH)

    zh_copy = pltpu.make_async_remote_copy(
        z_part, z_half, zhs_sem, zhr_sem, device_id=mate, device_id_type=MESH)

    pl.semaphore_wait(barrier, NDIM + 1)

    def far(q, carry):
        front(oth0 + q * gsz)
        half_copy(q).start()
        return carry

    lax.fori_loop(0, NDIM, far, 0)
    for cp in wi_copies + wo_copies:
        cp.start()

    for q in range(NDIM):
        front(own0 + q * gsz)
        half_copy(q).wait_recv()
        for k in range(nk):
            for u in range(gsz):
                b = own0 + q * gsz + u
                part[k, b] = (part[k, b].astype(F32) + half_in[k, q * gsz + u].astype(F32)).astype(BF16)
            rs_copy(k, q, 0).start()

    zh_copy.start()
    zh_copy.wait()
    z_part[...] += z_half[...]
    z_copy(0).start()

    def flip_c(b, carry):
        c_v[b] = ct_v[b].astype(F32).T.astype(BF16)
        return carry

    lax.fori_loop(0, rows, flip_c, 0)

    def rs_add(k, q, s):
        order = orders[q]
        rs_copy(k, q, s).wait()
        for u in range(gsz):
            at = (k, own0 + q * gsz + u) + where_(order, s + 1, False)
            part[at] = (part[at].astype(F32) + rbuf[s][k, q * gsz + u].astype(F32)).astype(BF16)

    for s in range(NDIM - 1):
        for k in range(nk):
            for q in range(NDIM):
                rs_add(k, q, s)
                rs_copy(k, q, s + 1).start()
        z_copy(s).wait()
        at = where_(orders[0], s + 1, False)
        z_part[at] = z_part[at] + zbuf[s][...]
        z_copy(s + 1).start()

    z_copy(3).wait()
    z_own = z_part[bits] + z3[...]
    z_lane = lax.broadcasted_iota(jnp.int32, z_own.shape, 1)
    z_inv = [
        1.0 / jnp.sum(jnp.where(z_lane == own0 + j, z_own, 0.0), axis=1, keepdims=True)
        for j in range(hrows)
    ]

    def xs_copy(k):
        ref = xs.at[k, pl.ds(own0, hrows)]
        return pltpu.make_async_remote_copy(
            ref, ref, xss_sem.at[k], xsr_sem.at[k], device_id=mate, device_id_type=MESH)

    def ffn_in(k):
        xs_copy(k).wait()
        for t in range(CHUNK // 128):
            xs_f[t] = xs[k, :, :, t * 128:(t + 1) * 128].astype(F32).reshape(rows * chip_rows, 128)
        for e in range(experts):
            if k == 0:
                wi_copies[e].wait()
            pick = pl.ds(core * experts + e, rows, stride=chip_rows)
            xe = jnp.concatenate([xs_f[t, pick, :] for t in range(CHUNK // 128)], axis=1).astype(BF16)
            h = _nn(xe, wi_v[e, k * CHUNK:(k + 1) * CHUNK, :])
            hid[e] = h if k == 0 else hid[e] + h

    for k in range(nk):
        for q in range(NDIM):
            rs_copy(k, q, 3).wait()
            for u in range(gsz):
                j = q * gsz + u
                s_own = part[(k, own0 + j) + bits].astype(F32) + r3[k, j].astype(F32)
                xs[k, own0 + j] = (s_own * z_inv[j]).astype(BF16)
        xs_copy(k).start()
        if k > 0:
            ffn_in(k - 1)
    ffn_in(nk - 1)
    for e in range(experts):
        hid_b[e] = jax.nn.gelu(hid[e], approximate=True).astype(BF16)

    row8 = lax.broadcasted_iota(jnp.int32, (hrows, chip_rows, CHUNK), 1)
    mine8 = (row8 // experts) == core

    def yx_copy(k):
        return pltpu.make_async_remote_copy(
            yx.at[k, pl.ds(oth0, hrows)], yx_in.at[k],
            yxs_sem.at[k], yxr_sem.at[k], device_id=mate, device_id_type=MESH)

    def g_copy(k, q, s):
        order = orders[q]
        i = (k * NDIM + q) * NDIM + s
        ref = gath.at[(k, pl.ds(own0 + q * gsz, gsz)) + where_(order, s + 1, False)]
        return pltpu.make_async_remote_copy(
            ref, ref, gs_sem.at[i], gr_sem.at[i], device_id=flips[order[s]], device_id_type=MESH)

    def gd_copy(k, q):
        ref = gath.at[k, pl.ds(own0 + q * gsz, gsz)]
        i = k * NDIM + q
        return pltpu.make_async_remote_copy(
            ref, ref, gds_sem.at[i], gdr_sem.at[i], device_id=mate, device_id_type=MESH)

    def ffn_out(k):
        for e in range(experts):
            if k == 0:
                wo_copies[e].wait()
            ye = _nn(hid_b[e], wo_v[e, :, k * CHUNK:(k + 1) * CHUNK])
            for t in range(CHUNK // 128):
                ys_f[t, pl.ds(core * experts + e, rows, stride=chip_rows), :] = ye[:, t * 128:(t + 1) * 128]
        for t in range(CHUNK // 128):
            yx[k, :, :, t * 128:(t + 1) * 128] = ys_f[t].reshape(rows, chip_rows, 128).astype(BF16)
        yx_copy(k).start()

    def merge(k):
        yx_copy(k).wait()
        own = yx[k, pl.ds(own0, hrows)].astype(F32)
        merged = jnp.where(mine8, own, yx_in[k].astype(F32)).astype(BF16)
        gath[(k, pl.ds(own0, hrows)) + bits] = merged
        for q in range(NDIM):
            g_copy(k, q, NDIM - 1).start()

    for k in range(nk):
        ffn_out(k)
        if k > 0:
            merge(k - 1)
    merge(nk - 1)

    for s in range(NDIM - 1, 0, -1):
        for k in range(nk):
            for q in range(NDIM):
                g_copy(k, q, s).wait()
                g_copy(k, q, s - 1).start()

    row_pos = me * tok_count + lax.broadcasted_iota(jnp.int32, (tok_count, CHUNK), 0)

    def mix(k, b0):
        for u in range(gsz):
            b = b0 + u
            gb = gath[k, b].astype(F32).reshape(nslots, CHUNK).astype(BF16)
            yk = jnp.where(row_pos < len_ref[b], _nn(c_v[b], gb), 0.0)
            x_v[b, :, k * CHUNK:(k + 1) * CHUNK] = yk.astype(BF16)

    def out_copy(b):
        return pltpu.make_async_copy(x_v.at[b], y_hbm.at[b], out_sem.at[b])

    for k in range(nk):
        for q in range(NDIM):
            g_copy(k, q, 0).wait()
            gd_copy(k, q).start()
            mix(k, own0 + q * gsz)
            if k == nk - 1:
                for u in range(gsz):
                    out_copy(own0 + q * gsz + u).start()
    for k in range(nk):
        for q in range(NDIM):
            gd_copy(k, q).wait()
            mix(k, oth0 + q * gsz)
            if k == nk - 1:
                for u in range(gsz):
                    out_copy(oth0 + q * gsz + u).start()
    for q in range(NDIM):
        half_copy(q).wait_send()
    for b in range(rows):
        out_copy(b).wait()


def solution(mesh):
    def shard_body(tok, lens, phi, gain, w_in, w_out):
        rows, tok_count, width = tok.shape
        experts, _, ff = w_in.shape
        nslots = phi.shape[1]
        nk = width // CHUNK
        hrows = rows // 2
        cr = 2 * experts
        cube = (2, 2, 2, 2)
        vm = pltpu.VMEM
        dma = pltpu.SemaphoreType.DMA
        anyspace = pl.BlockSpec(memory_space=pl.ANY)
        smem = pl.BlockSpec(memory_space=pltpu.SMEM)
        scratch = [
            vm((rows, tok_count, width), BF16),
            vm((width, nslots), BF16),
            vm((nslots, width), BF16),
            vm(w_in.shape, BF16),
            vm(w_out.shape, BF16),
            vm((rows, nslots, tok_count), BF16),
            vm((rows, tok_count, nslots), BF16),
            vm((nk, rows) + cube + (cr, CHUNK), BF16),
            vm((nk, hrows) + cube + (cr, CHUNK), BF16),
            vm((nk, hrows, 2, 2, 2, cr, CHUNK), BF16),
            vm((nk, hrows, 2, 2, cr, CHUNK), BF16),
            vm((nk, hrows, 2, cr, CHUNK), BF16),
            vm((nk, hrows, cr, CHUNK), BF16),
            vm(cube + (cr, tok_count), F32),
            vm(cube + (cr, tok_count), F32),
            vm((2, 2, 2, cr, tok_count), F32),
            vm((2, 2, cr, tok_count), F32),
            vm((2, cr, tok_count), F32),
            vm((cr, tok_count), F32),
            vm((nk, rows, cr, CHUNK), BF16),
            vm((CHUNK // 128, rows * cr, 128), F32),
            vm((experts, rows, ff), F32),
            vm((experts, rows, ff), BF16),
            vm((CHUNK // 128, rows * cr, 128), F32),
            vm((nk, rows, cr, CHUNK), BF16),
            vm((nk, hrows, cr, CHUNK), BF16),
            vm((nk, rows) + cube + (cr, CHUNK), BF16),
            dma((rows,)), dma, dma((experts,)), dma((experts,)), dma((rows,)),
            dma((NDIM,)), dma((NDIM,)), dma, dma, dma((NDIM,)), dma((NDIM,)),
            dma((nk * NDIM * NDIM,)), dma((nk * NDIM * NDIM,)),
            dma((nk,)), dma((nk,)), dma((nk,)), dma((nk,)),
            dma((nk * NDIM * NDIM,)), dma((nk * NDIM * NDIM,)),
            dma((nk * NDIM,)), dma((nk * NDIM,)),
        ]
        return pl.pallas_call(
            _kernel,
            out_shape=jax.ShapeDtypeStruct(tok.shape, BF16),
            in_specs=[smem, smem, anyspace, anyspace, anyspace, anyspace],
            out_specs=anyspace,
            scratch_shapes=scratch,
            compiler_params=pltpu.CompilerParams(
                collective_id=0, has_side_effects=True, vmem_limit_bytes=67043328),
        )(lens, gain, tok, phi, w_in, w_out)

    return jax.shard_map(
        shard_body,
        mesh=mesh,
        in_specs=(P("data", "seq", None), P("data"), P(None, None), P(None), P("seq", None, None), P("seq", None, None)),
        out_specs=P("data", "seq", None),
        check_vma=False,
    )
```

time: 210 us -> 66.9 us (0.32)
  blocking collectives: 93.9 us -> 0 us
  waiting for transfers between devices: 64.5 us -> 0 us
  Pallas kernels: 0 us -> 62.3 us
  matrix products: 27.6 us -> 0 us
  between operations: 14.1 us -> 0.66 us
  other arithmetic: 4.88 us -> 0 us
    pallas_call x0 -> x1, Pallas kernels: none -> 62.3 us  [shard_body(): pl.pallas_call(_kernel, out_shape=jax.ShapeDtypeStruct(tok.shape, BF16),...]
    pmax x1 -> x0, blocking collectives: 49.8 us -> none  [shard_body(): col_max = lax.pmax(local_max, 'seq')]
    psum x1 -> x0, blocking collectives: 44.1 us -> none  [shard_body(): col_sum = lax.psum(jnp.sum(disp_w, axis=1), 'seq')]
    all_gather x1 -> x0, waiting for transfers between devices: 40.6 us -> none  [shard_body(): all_out = lax.all_gather(slot_out, 'seq', axis=1, tiled=True)]
    dot_general x4 -> x0, matrix products: 27.6 us -> none  [the longest x1 15 us: shard_body(): jnp.einsum('besf,efd->besd', hidden, w_out_blk, preferred_element_type=jn...]
    reduce_scatter x1 -> x0, waiting for transfers between devices: 23.8 us -> none  [shard_body(): lax.psum_scatter(part_sum, 'seq', scatter_dimension=1, tiled=True)]
    reduce_sum x3 -> x0, other arithmetic: 4.16 us -> none  [the longest x1 2.73 us: shard_body(): jnp.sum(tok_f32 * tok_f32, axis=-1, keepdims=True) + 1e-06]
    dot_general x1 -> x0, local copies, waits for them, and re-layouts: 3.4 us -> none  [shard_body(): jnp.einsum('btn,btd->bnd', disp_w.astype(jnp.bfloat16), tok_blk, preferre...]
  transfers between devices with their start and end apart: 2 -> 0, of which waited for: 2 -> 0; matrix products, arithmetic and copies ran while one was open for 1% -> 0% of each run, Pallas kernels for 0% -> 0%
where the time goes in v1:
time: 66.9 us; the launch traced here: 66.8 us
  Pallas kernels  62.3 us (93%)
  local copies, waits for them, and re-layouts  3.83 us (6%)
    pallas_call x1, Pallas kernels, shard_body(): pl.pallas_call(_kernel, out_shape=jax.ShapeDtypeStruct(tok.shape, BF16),...  62.3 us
    unnamed x1, local copies, waits for them, and re-layouts  3.83 us

profile of v1, /device:TPU:97, one launch (start us, length us, event | category | flops | bytes accessed | tf_op | source)
XLA Modules:
  0.0 66.8 jit_solution(9391477100006422901)
XLA Ops:
  0.7 62.3 %shard_map.64 = bf16[16,128,768]{2,1,0:T(8,128)(2,1)} custom-call(s32[16]{0:T(128)} %len_ref.1, f32[1]{0:T(128)S(6)} %copy.8.gain_ref, bf16[16,128,768]{2,1,0:T(8,128)(2,1)} %tok_hbm.1, bf16[768,128]{1,0:T(8,128)(2,1)} %phi_hbm.1, bf16[4,768,3072]{2,1,0:T(8,128)(2,1)} %wi_hbm.1, bf16[4,3072,768]{2,1,0:T(8,128)(2,1)} %wo_hbm.1), custom_call_target="tpu_custom_call" | custom-call | tf_op jit(solution)/shard_map/pallas_call | solution.py:367
  63.0 3.8 %copy.9 = bf16[16,128,768]{2,1,0:T(8,128)(2,1)} copy(bf16[16,128,768]{2,1,0:T(8,128)(2,1)} %shard_map.64) | data formatting | bytes 6291456

commit v2 on v0

v2 whole, which is shorter than its diff:
```python
import functools

import jax
import jax.numpy as jnp
from jax import lax
from jax.experimental import pallas as pl
from jax.experimental.pallas import tpu as pltpu
from jax.sharding import PartitionSpec as P

CHUNK = 256
GROUPS = 4
F32 = jnp.float32
BF16 = jnp.bfloat16
MESH = pl.DeviceIdType.MESH
ORDERS = ((3, 1, 2, 0), (1, 2, 3, 0), (2, 0, 3, 1), (0, 3, 2, 1))
FLIPS = tuple((f & 1, (f >> 1) & 1, (f >> 2) & 1) for f in range(1, 8))


def _nt(a, b):
    return lax.dot_general(a, b, (((1,), (1,)), ((), ())), preferred_element_type=F32)


def _nn(a, b):
    return jnp.dot(a, b, preferred_element_type=F32)


def _exchange_kernel(len_ref, gain_ref, tok_hbm, phi_hbm, wi_hbm, wo_hbm, g_hbm, c_hbm,
                     x_v, xn_v, w_v, phi_v, phit_v, wi_v, wo_v, ct_v, c_v, part, half_in, r0, r1, q_out, q_in,
                     z_part, z_half, z0, z1, zq, xs_f, hid, hid_b, ys_f, yx, g_in, gath,
                     phi_sem, tok_sem, wi_sem, wo_sem, c_sem,
                     hs_sem, hr_sem, zhs_sem, zhr_sem, zs_sem, zr_sem, rs_sem, rr_sem,
                     qs_sem, qr_sem, ys_sem, yr_sem, gs_sem, gr_sem, gds_sem, gdr_sem, go_sem):
    rows, tok_count, width = x_v.shape
    experts = wi_v.shape[0]
    nk = width // CHUNK
    hrows = rows // 2
    gsz = hrows // GROUPS
    nslots = phit_v.shape[0]
    chip_rows = 2 * experts
    me = lax.axis_index("seq")
    core = lax.rem(me, 2)
    chip = me // 2
    x = lax.rem(chip, 4)
    y = chip // 4
    xb = x // 2
    xa = lax.rem(x + xb, 2)
    yb = y // 2
    ya = lax.rem(y + yb, 2)
    bits = (yb, ya, xb, xa)

    def peer(dims, flip_core=0):
        b = [1 - v if d in dims else v for d, v in enumerate(bits)]
        yy = 2 * b[0] + lax.rem(b[0] + b[1], 2)
        xx = 2 * b[2] + lax.rem(b[2] + b[3], 2)
        return {"seq": (yy * 4 + xx) * 2 + (1 - core if flip_core else core)}

    def group_peer(q, f):
        fu, fv, fc = FLIPS[f]
        dims = tuple(d for d, on in zip(ORDERS[q][2:], (fu, fv)) if on)
        return peer(dims, fc)

    mate = peer((), 1)
    steps = tuple(peer((d,)) for d in range(4))
    own0 = core * hrows
    oth0 = (1 - core) * hrows

    pairs = sorted({dims for q in range(GROUPS) for dims in (tuple(sorted(ORDERS[q][2:])),)})
    greet = []
    for fc in (0, 1):
        greet += [peer((d,), fc) for d in range(4)]
        greet += [peer(dims, fc) for dims in pairs]
    greet.append(mate)
    barrier = pltpu.get_barrier_semaphore()
    for d in greet:
        pl.semaphore_signal(barrier, inc=1, device_id=d, device_id_type=MESH)

    def tok_copy(h):
        at = pl.ds(oth0 if h == 0 else own0, hrows)
        return pltpu.make_async_copy(tok_hbm.at[at], x_v.at[at], tok_sem.at[h])

    phi_copy = pltpu.make_async_copy(phi_hbm, phi_v, phi_sem)
    wi_copies = [pltpu.make_async_copy(wi_hbm.at[e], wi_v.at[e], wi_sem.at[e]) for e in range(experts)]
    wo_copies = [pltpu.make_async_copy(wo_hbm.at[e], wo_v.at[e], wo_sem.at[e]) for e in range(experts)]
    phi_copy.start()
    tok_copy(0).start()
    tok_copy(1).start()

    z_part[...] = jnp.zeros_like(z_part)
    gain = gain_ref[0]
    shift = gain * (1.0 + 2.0 ** -7)
    lane = lax.broadcasted_iota(jnp.int32, (nslots, tok_count), 1)
    pos = me * tok_count + lane

    def batch(i):
        return oth0 + i if i < hrows else own0 + i - hrows

    def normalise(i):
        xf = x_v[batch(i)].astype(F32)
        xn_v[i] = (xf * lax.rsqrt(jnp.sum(xf * xf, axis=1, keepdims=True) + 1e-6)).astype(BF16)

    def weigh(i):
        b = batch(i)
        ex = jnp.exp(_nt(phit_v[...], xn_v[i]) - shift)
        ct_v[b] = (ex * (1.0 / jnp.sum(ex, axis=0, keepdims=True))).astype(BF16)
        exm = jnp.where(pos < len_ref[b], ex, 0.0)
        w_v[i] = exm.astype(BF16)
        zs = jnp.where(lane == b, jnp.sum(exm, axis=1, keepdims=True), 0.0)
        z_part[...] += zs.reshape(z_part.shape)

    def collect(i):
        b = batch(i)
        for k in range(nk):
            pk = _nn(w_v[i], x_v[b, :, k * CHUNK:(k + 1) * CHUNK])
            part[k, b] = pk.reshape(2, 2, 2, 2, chip_rows, CHUNK).astype(BF16)

    def half_copy(q):
        return pltpu.make_async_remote_copy(
            part.at[:, pl.ds(oth0 + q * gsz, gsz)], half_in.at[:, pl.ds(q * gsz, gsz)],
            hs_sem.at[q], hr_sem.at[q], device_id=mate, device_id_type=MESH)

    def region(order, fixed, flip=None):
        idx = [slice(None)] * 4
        for t in range(fixed):
            idx[order[t]] = bits[order[t]]
        if flip is not None:
            idx[flip] = 1 - bits[flip]
        return tuple(idx)

    rbuf = (r0, r1)
    zbuf = (z0, z1)

    def rs_copy(k, q, s):
        order = ORDERS[q]
        i = (k * GROUPS + q) * 2 + s
        return pltpu.make_async_remote_copy(
            part.at[(k, pl.ds(own0 + q * gsz, gsz)) + region(order, s, order[s])],
            rbuf[s].at[k, pl.ds(q * gsz, gsz)],
            rs_sem.at[i], rr_sem.at[i], device_id=steps[order[s]], device_id_type=MESH)

    def z_copy(s):
        order = ORDERS[0]
        return pltpu.make_async_remote_copy(
            z_part.at[region(order, s, order[s])], zbuf[s],
            zs_sem.at[s], zr_sem.at[s], device_id=steps[order[s]], device_id_type=MESH)

    def zq_copy(f):
        fu, fv, _ = FLIPS[f]
        order = ORDERS[0]
        idx = list(bits)
        for d, on in zip(order[2:], (fu, fv)):
            if on:
                idx[d] = 1 - idx[d]
        return pltpu.make_async_remote_copy(
            z_part.at[tuple(idx)], zq.at[f], zs_sem.at[2 + f], zr_sem.at[2 + f],
            device_id=group_peer(0, f), device_id_type=MESH)

    zh_copy = pltpu.make_async_remote_copy(
        z_part, z_half, zhs_sem, zhr_sem, device_id=mate, device_id_type=MESH)

    phi_copy.wait()
    pf = phi_v[...].astype(F32)
    pn = (pf * (gain * lax.rsqrt(jnp.sum(pf * pf, axis=0, keepdims=True) + 1e-6))).astype(BF16)
    new = lax.broadcasted_iota(jnp.int32, (nslots, nslots), 0)
    old = lax.broadcasted_iota(jnp.int32, (nslots, nslots), 1)
    nchip = new // chip_rows
    nxa, nxb, nya, nyb = nchip & 1, (nchip >> 1) & 1, (nchip >> 2) & 1, (nchip >> 3) & 1
    src = ((2 * nyb + (nya ^ nyb)) * 4 + 2 * nxb + (nxa ^ nxb)) * chip_rows + (new & (chip_rows - 1))
    perm = jnp.where(src == old, 1.0, 0.0).astype(BF16)
    phit_v[...] = _nt(perm, pn).astype(BF16)

    tok_copy(0).wait()
    for cp in wi_copies + wo_copies:
        cp.start()
    for i in range(hrows + 2):
        if i < hrows:
            normalise(i)
        if 1 <= i < hrows + 1:
            weigh(i - 1)
        if i >= 2:
            collect(i - 2)
    pl.semaphore_wait(barrier, len(greet))
    for q in range(GROUPS):
        half_copy(q).start()
    tok_copy(1).wait()
    for i in range(hrows, rows + 2):
        if i < rows:
            normalise(i)
        if hrows + 1 <= i < rows + 1:
            weigh(i - 1)
        if i >= hrows + 2:
            collect(i - 2)
    zh_copy.start()

    for q in range(GROUPS):
        half_copy(q).wait_recv()
        for k in range(nk):
            for u in range(gsz):
                b = own0 + q * gsz + u
                part[k, b] = (part[k, b].astype(F32) + half_in[k, q * gsz + u].astype(F32)).astype(BF16)
            rs_copy(k, q, 0).start()

    zh_copy.wait()
    z_part[...] += z_half[...]
    z_copy(0).start()


    def flip_c(i, carry):
        for u in range(4):
            c_v[4 * i + u] = ct_v[4 * i + u].astype(F32).T.astype(BF16)
        return carry

    lax.fori_loop(0, rows // 4, flip_c, 0)
    c_copy = pltpu.make_async_copy(c_v, c_hbm, c_sem)
    c_copy.start()

    def q_copy(k, q, f):
        fu, fv, fc = FLIPS[f]
        o = ORDERS[q]
        mu, mv = bits[o[2]], bits[o[3]]
        du = 1 - mu if fu else mu
        dv = 1 - mv if fv else mv
        dc = 1 - core if fc else core
        i = (k * GROUPS + q) * 7 + f
        return pltpu.make_async_remote_copy(
            q_out.at[k, q, dc, du, dv], q_in.at[k, q, core, mu, mv],
            qs_sem.at[i], qr_sem.at[i], device_id=group_peer(q, f), device_id_type=MESH)

    row8 = lax.broadcasted_iota(jnp.int32, (chip_rows, CHUNK), 0)
    low = row8 < experts

    def at_rest(q, u, v):
        o = ORDERS[q]
        idx = list(bits)
        idx[o[2]] = u
        idx[o[3]] = v
        return tuple(idx)

    def at_recv(q, u, v):
        o = ORDERS[q]
        free = sorted(o[2:])
        val = {o[2]: u, o[3]: v}
        return tuple(val[d] for d in free)

    for k in range(nk):
        for q in range(GROUPS):
            o = ORDERS[q]
            rs_copy(k, q, 0).wait()
            for u in range(gsz):
                at = (k, own0 + q * gsz + u) + region(o, 1)
                part[at] = (part[at].astype(F32) + r0[k, q * gsz + u].astype(F32)).astype(BF16)
            rs_copy(k, q, 1).start()
    z_copy(0).wait()
    at = region(ORDERS[0], 1)
    z_part[at] = z_part[at] + z0[...]
    z_copy(1).start()
    for k in range(nk):
        for q in range(GROUPS):
            o = ORDERS[q]
            mu, mv = bits[o[2]], bits[o[3]]
            rs_copy(k, q, 1).wait()
            for u in range(2):
                for v in range(2):
                    ev, od = [
                        part[(k, own0 + q * gsz + w) + at_rest(q, u, v)].astype(F32)
                        + r1[(k, q * gsz + w) + at_recv(q, u, v)].astype(F32)
                        for w in range(gsz)
                    ]
                    q_out[k, q, 0, u, v] = jnp.where(low, ev, pltpu.roll(od, experts, 0)).astype(BF16)
                    q_out[k, q, 1, u, v] = jnp.where(low, pltpu.roll(ev, experts, 0), od).astype(BF16)
            for f in range(7):
                q_copy(k, q, f).start()
            q_in[k, q, core, mu, mv] = q_out[k, q, core, mu, mv]
    z_copy(1).wait()
    at = region(ORDERS[0], 2)
    z_part[at] = z_part[at] + z1[...]
    for f in range(3):
        zq_copy(f).start()
    for f in range(3):
        zq_copy(f).wait()
    z_own = z_part[bits] + (zq[0] + (zq[1] + zq[2]))
    zrow = lax.broadcasted_iota(jnp.int32, z_own.shape, 0)
    eye = lax.broadcasted_iota(jnp.int32, (rows, z_own.shape[1]), 0) == lax.broadcasted_iota(
        jnp.int32, (rows, z_own.shape[1]), 1)
    z_inv = []
    for e in range(experts):
        zr = jnp.sum(jnp.where(zrow == core * experts + e, z_own, 0.0), axis=0, keepdims=True)
        z_inv.append(1.0 / jnp.sum(jnp.where(eye, zr, 0.0), axis=1, keepdims=True))

    lanes = CHUNK // 128
    for cp in wi_copies:
        cp.wait()
    for k in range(nk):
        for q in range(GROUPS):
            for f in range(7):
                q_copy(k, q, f).wait()
        for cs in range(2):
            for q in range(GROUPS):
                p = cs * GROUPS + q
                s = [q_in[k, q, cs, u, v].astype(F32) for u in range(2) for v in range(2)]
                s = (s[0] + s[1]) + (s[2] + s[3])
                for t in range(lanes):
                    xs_f[t, p * chip_rows:(p + 1) * chip_rows, :] = s[:, t * 128:(t + 1) * 128]
        for e in range(experts):
            pick = pl.ds(e, rows, stride=experts)
            xe = jnp.concatenate([xs_f[t, pick, :] for t in range(lanes)], axis=1)
            h = _nn((xe * z_inv[e]).astype(BF16), wi_v[e, k * CHUNK:(k + 1) * CHUNK, :])
            hid[e] = h if k == 0 else hid[e] + h
    for cp in wo_copies:
        cp.wait()
    for e in range(experts):
        hid_b[e] = jax.nn.gelu(hid[e], approximate=True).astype(BF16)

    def y_copy(k, q, f):
        _, _, fc = FLIPS[f]
        o = ORDERS[q]
        dc = 1 - core if fc else core
        i = (k * GROUPS + q) * 7 + f
        return pltpu.make_async_remote_copy(
            yx.at[k, dc * GROUPS + q], g_in.at[k, q, core, bits[o[2]], bits[o[3]]],
            ys_sem.at[i], yr_sem.at[i], device_id=group_peer(q, f), device_id_type=MESH)

    def g_copy(k, q, s):
        i = (k * GROUPS + q) * 2 + s
        ref = gath.at[(k, pl.ds(own0 + q * gsz, gsz)) + region(ORDERS[q], s + 1)]
        return pltpu.make_async_remote_copy(
            ref, ref, gs_sem.at[i], gr_sem.at[i], device_id=steps[ORDERS[q][s]], device_id_type=MESH)

    def gd_copy(k, q):
        at = (k, pl.ds(own0 + q * gsz, gsz))
        i = k * GROUPS + q
        return pltpu.make_async_remote_copy(
            gath.at[at], g_hbm.at[at], gds_sem.at[i], gdr_sem.at[i], device_id=mate, device_id_type=MESH)

    def go_copy(k, q):
        at = (k, pl.ds(own0 + q * gsz, gsz))
        return pltpu.make_async_copy(gath.at[at], g_hbm.at[at], go_sem.at[k * GROUPS + q])

    for k in range(nk):
        for e in range(experts):
            ye = _nn(hid_b[e], wo_v[e, :, k * CHUNK:(k + 1) * CHUNK])
            for t in range(lanes):
                ys_f[t, pl.ds(e, rows, stride=experts), :] = ye[:, t * 128:(t + 1) * 128]
        for t in range(lanes):
            yx[k, :, :, t * 128:(t + 1) * 128] = ys_f[t].reshape(rows // 2, chip_rows, 128).astype(BF16)
        for q in range(GROUPS):
            o = ORDERS[q]
            for f in range(7):
                y_copy(k, q, f).start()
            g_in[k, q, core, bits[o[2]], bits[o[3]]] = yx[k, core * GROUPS + q]

    for k in range(nk):
        for q in range(GROUPS):
            for f in range(7):
                y_copy(k, q, f).wait()
            for u in range(2):
                for v in range(2):
                    s0 = g_in[k, q, 0, u, v].astype(F32)
                    s1 = g_in[k, q, 1, u, v].astype(F32)
                    at = at_rest(q, u, v)
                    gath[(k, own0 + q * gsz) + at] = jnp.where(low, s0, pltpu.roll(s1, experts, 0)).astype(BF16)
                    gath[(k, own0 + q * gsz + 1) + at] = jnp.where(low, pltpu.roll(s0, experts, 0), s1).astype(BF16)
            g_copy(k, q, 1).start()
    for k in range(nk):
        for q in range(GROUPS):
            g_copy(k, q, 1).wait()
            g_copy(k, q, 0).start()
    for k in range(nk):
        for q in range(GROUPS):
            g_copy(k, q, 0).wait()
            gd_copy(k, q).start()
            go_copy(k, q).start()
    for k in range(nk):
        for q in range(GROUPS):
            gd_copy(k, q).wait()
            go_copy(k, q).wait()
    for q in range(GROUPS):
        half_copy(q).wait_send()
    c_copy.wait()


def _mix_kernel(len_ref, g_hbm, c_hbm, y_hbm, g_v, c_v, y_v, g_sem, c_sem, y_sem):
    rows, tok_count, width = y_v.shape
    nk = g_v.shape[0]
    nslots = c_v.shape[2]

    def c_copy(b):
        return pltpu.make_async_copy(c_hbm.at[b], c_v.at[b], c_sem.at[b])

    def g_copy(b):
        return pltpu.make_async_copy(g_hbm.at[:, b], g_v.at[:, b], g_sem.at[b])

    def y_copy(b):
        return pltpu.make_async_copy(y_v.at[b], y_hbm.at[b], y_sem.at[b])

    for b in range(rows):
        c_copy(b).start()
        g_copy(b).start()
    row_pos = lax.axis_index("seq") * tok_count + lax.broadcasted_iota(jnp.int32, (tok_count, CHUNK), 0)
    for b0 in range(0, rows, 2):
        for b in (b0, b0 + 1):
            c_copy(b).wait()
            g_copy(b).wait()
        for b in (b0, b0 + 1):
            for k in range(nk):
                gb = g_v[k, b].astype(F32).reshape(nslots, CHUNK).astype(BF16)
                yk = jnp.where(row_pos < len_ref[b], _nn(c_v[b], gb), 0.0)
                y_v[b, :, k * CHUNK:(k + 1) * CHUNK] = yk.astype(BF16)
        for b in (b0, b0 + 1):
            y_copy(b).start()
    for b in range(rows):
        y_copy(b).wait()


def solution(mesh):
    def shard_body(tok, lens, phi, gain, w_in, w_out):
        rows, tok_count, width = tok.shape
        experts, _, ff = w_in.shape
        nslots = phi.shape[1]
        nk = width // CHUNK
        hrows = rows // 2
        cr = 2 * experts
        cube = (2, 2, 2, 2)
        tile = (cr, CHUNK)
        lanes = CHUNK // 128
        vm = pltpu.VMEM
        dma = pltpu.SemaphoreType.DMA
        anyspace = pl.BlockSpec(memory_space=pl.ANY)
        smem = pl.BlockSpec(memory_space=pltpu.SMEM)
        gshape = (nk, rows) + cube + tile
        scratch = [
            vm((rows, tok_count, width), BF16),
            vm((rows, tok_count, width), BF16),
            vm((rows, nslots, tok_count), BF16),
            vm((width, nslots), BF16),
            vm((nslots, width), BF16),
            vm(w_in.shape, BF16),
            vm(w_out.shape, BF16),
            vm((rows, nslots, tok_count), BF16),
            vm((rows, tok_count, nslots), BF16),
            vm(gshape, BF16),
            vm((nk, hrows) + cube + tile, BF16),
            vm((nk, hrows, 2, 2, 2) + tile, BF16),
            vm((nk, hrows, 2, 2) + tile, BF16),
            vm((nk, GROUPS, 2, 2, 2) + tile, BF16),
            vm((nk, GROUPS, 2, 2, 2) + tile, BF16),
            vm(cube + (cr, tok_count), F32),
            vm(cube + (cr, tok_count), F32),
            vm((2, 2, 2, cr, tok_count), F32),
            vm((2, 2, cr, tok_count), F32),
            vm((3, cr, tok_count), F32),
            vm((lanes, rows * experts, 128), F32),
            vm((experts, rows, ff), F32),
            vm((experts, rows, ff), BF16),
            vm((lanes, rows * experts, 128), F32),
            vm((nk, rows // 2) + tile, BF16),
            vm((nk, GROUPS, 2, 2, 2) + tile, BF16),
            vm(gshape, BF16),
            dma, dma((2,)), dma((experts,)), dma((experts,)), dma,
            dma((GROUPS,)), dma((GROUPS,)), dma, dma, dma((5,)), dma((5,)),
            dma((nk * GROUPS * 2,)), dma((nk * GROUPS * 2,)),
            dma((nk * GROUPS * 7,)), dma((nk * GROUPS * 7,)),
            dma((nk * GROUPS * 7,)), dma((nk * GROUPS * 7,)),
            dma((nk * GROUPS * 2,)), dma((nk * GROUPS * 2,)),
            dma((nk * GROUPS,)), dma((nk * GROUPS,)), dma((nk * GROUPS,)),
        ]
        gath, comb = pl.pallas_call(
            _exchange_kernel,
            out_shape=(
                jax.ShapeDtypeStruct(gshape, BF16),
                jax.ShapeDtypeStruct((rows, tok_count, nslots), BF16),
            ),
            in_specs=[smem, smem, anyspace, anyspace, anyspace, anyspace],
            out_specs=(anyspace, anyspace),
            scratch_shapes=scratch,
            compiler_params=pltpu.CompilerParams(
                collective_id=0, has_side_effects=True, vmem_limit_bytes=67043328),
        )(lens, gain, tok, phi, w_in, w_out)
        return pl.pallas_call(
            _mix_kernel,
            out_shape=jax.ShapeDtypeStruct(tok.shape, BF16),
            in_specs=[smem, anyspace, anyspace],
            out_specs=anyspace,
            scratch_shapes=[
                vm(gshape, BF16),
                vm((rows, tok_count, nslots), BF16),
                vm(tok.shape, BF16),
                dma((rows,)), dma((rows,)), dma((rows,)),
            ],
        )(lens, gath, comb)

    return jax.shard_map(
        shard_body,
        mesh=mesh,
        in_specs=(P("data", "seq", None), P("data"), P(None, None), P(None), P("seq", None, None), P("seq", None, None)),
        out_specs=P("data", "seq", None),
        check_vma=False,
    )
```

time: 210 us -> 58.8 us (0.28)
  blocking collectives: 93.9 us -> 0 us
  waiting for transfers between devices: 64.5 us -> 0 us
  Pallas kernels: 0 us -> 57.8 us
  matrix products: 27.6 us -> 0 us
  between operations: 14.1 us -> 0.82 us
  other arithmetic: 4.88 us -> 0 us
  local copies, waits for them, and re-layouts: 4.66 us -> 0 us
    pallas_call x0 -> x2, Pallas kernels: none -> 57.8 us  [the longest x1 52.9 us: shard_body(): pl.pallas_call(_exchange_kernel, out_shape=(jax.ShapeDtypeStruct(gshape,...]
    pmax x1 -> x0, blocking collectives: 49.8 us -> none  [shard_body(): col_max = lax.pmax(local_max, 'seq')]
    psum x1 -> x0, blocking collectives: 44.1 us -> none  [shard_body(): col_sum = lax.psum(jnp.sum(disp_w, axis=1), 'seq')]
    all_gather x1 -> x0, waiting for transfers between devices: 40.6 us -> none  [shard_body(): all_out = lax.all_gather(slot_out, 'seq', axis=1, tiled=True)]
    dot_general x4 -> x0, matrix products: 27.6 us -> none  [the longest x1 15 us: shard_body(): jnp.einsum('besf,efd->besd', hidden, w_out_blk, preferred_element_type=jn...]
    reduce_scatter x1 -> x0, waiting for transfers between devices: 23.8 us -> none  [shard_body(): lax.psum_scatter(part_sum, 'seq', scatter_dimension=1, tiled=True)]
    reduce_sum x3 -> x0, other arithmetic: 4.16 us -> none  [the longest x1 2.73 us: shard_body(): jnp.sum(tok_f32 * tok_f32, axis=-1, keepdims=True) + 1e-06]
    dot_general x1 -> x0, local copies, waits for them, and re-layouts: 3.4 us -> none  [shard_body(): jnp.einsum('btn,btd->bnd', disp_w.astype(jnp.bfloat16), tok_blk, preferre...]
  transfers between devices with their start and end apart: 2 -> 0, of which waited for: 2 -> 0; matrix products, arithmetic and copies ran while one was open for 1% -> 0% of each run, Pallas kernels for 0% -> 0%
where the time goes in v2:
time: 58.8 us; the launch traced here: 58.7 us
  Pallas kernels  57.8 us (98%)
  between operations  0.82 us (1%)
    pallas_call x1, Pallas kernels, shard_body(): pl.pallas_call(_exchange_kernel, out_shape=(jax.ShapeDtypeStruct(gshape,...  52.9 us
    pallas_call x1, Pallas kernels, shard_body(): pl.pallas_call(_mix_kernel, out_shape=jax.ShapeDtypeStruct(tok.shape, BF1...  4.95 us

profile of v2, /device:TPU:97, one launch (start us, length us, event | category | flops | bytes accessed | tf_op | source)
XLA Modules:
  0.0 58.7 jit_solution(926566022167663737)
XLA Ops:
  0.7 52.9 %shard_map.64 = (bf16[3,16,2,2,2,2,8,256]{7,6,5,4,3,2,1,0:T(8,128)(2,1)}, bf16[16,128,128]{2,1,0:T(8,128)(2,1)}) custom-call(s32[16]{0:T(128)} %len_ref.3, f32[1]{0:T(128)S(6)} %copy.7.gain_ref, bf16[16,128,768]{2,1,0:T(8,128)(2,1)} %tok_hbm.1, bf16[768,128]{1,0:T(8,128)(2,1)} %phi_hbm.1, bf16[4,768,3072]{2,1,0:T(8,128)(2,1)} %wi_hbm.1, ...), custom_call_target="tpu_custom_call" | custom-call | tf_op jit(solution)/shard_map/pallas_call | solution.py:466
  53.5 5.0 %shard_map.65 = bf16[16,128,768]{2,1,0:T(8,128)(2,1)} custom-call(s32[16]{0:T(128)} %len_ref.3, bf16[3,16,2,2,2,2,8,256]{7,6,5,4,3,2,1,0:T(8,128)(2,1)} %get-tuple-element.7.g_hbm, bf16[16,128,128]{2,1,0:T(8,128)(2,1)} %get-tuple-element.8.c_hbm), custom_call_target="tpu_custom_call" | custom-call | tf_op jit(solution)/shard_map/pallas_call | solution.py:478

commit v3 on v2

--- a/solution.py
+++ b/solution.py
@@ -12,7 +12,7 @@
 F32 = jnp.float32
 BF16 = jnp.bfloat16
 MESH = pl.DeviceIdType.MESH
-ORDERS = ((3, 1, 2, 0), (1, 2, 3, 0), (2, 0, 3, 1), (0, 3, 2, 1))
+ORDERS = ((3, 1, 2, 0), (1, 3, 2, 0), (2, 0, 3, 1), (0, 2, 3, 1))
 FLIPS = tuple((f & 1, (f >> 1) & 1, (f >> 2) & 1) for f in range(1, 8))
 
 
@@ -74,25 +74,26 @@
     for d in greet:
         pl.semaphore_signal(barrier, inc=1, device_id=d, device_id_type=MESH)
 
-    def tok_copy(h):
-        at = pl.ds(oth0 if h == 0 else own0, hrows)
-        return pltpu.make_async_copy(tok_hbm.at[at], x_v.at[at], tok_sem.at[h])
+    def batch(i):
+        q, r = divmod(i, 2 * gsz)
+        return (oth0 if r < gsz else own0 - gsz) + q * gsz + r
+
+    def tok_copy(i):
+        at = pl.ds(batch(i), gsz)
+        return pltpu.make_async_copy(tok_hbm.at[at], x_v.at[at], tok_sem.at[i // gsz])
 
     phi_copy = pltpu.make_async_copy(phi_hbm, phi_v, phi_sem)
     wi_copies = [pltpu.make_async_copy(wi_hbm.at[e], wi_v.at[e], wi_sem.at[e]) for e in range(experts)]
     wo_copies = [pltpu.make_async_copy(wo_hbm.at[e], wo_v.at[e], wo_sem.at[e]) for e in range(experts)]
     phi_copy.start()
-    tok_copy(0).start()
-    tok_copy(1).start()
+    for i in range(0, rows, gsz):
+        tok_copy(i).start()
 
     z_part[...] = jnp.zeros_like(z_part)
     gain = gain_ref[0]
     shift = gain * (1.0 + 2.0 ** -7)
     lane = lax.broadcasted_iota(jnp.int32, (nslots, tok_count), 1)
     pos = me * tok_count + lane
-
-    def batch(i):
-        return oth0 + i if i < hrows else own0 + i - hrows
 
     def normalise(i):
         xf = x_v[batch(i)].astype(F32)
@@ -168,36 +169,35 @@
     perm = jnp.where(src == old, 1.0, 0.0).astype(BF16)
     phit_v[...] = _nt(perm, pn).astype(BF16)
 
-    tok_copy(0).wait()
     for cp in wi_copies + wo_copies:
         cp.start()
-    for i in range(hrows + 2):
-        if i < hrows:
-            normalise(i)
-        if 1 <= i < hrows + 1:
-            weigh(i - 1)
-        if i >= 2:
-            collect(i - 2)
-    pl.semaphore_wait(barrier, len(greet))
-    for q in range(GROUPS):
-        half_copy(q).start()
-    tok_copy(1).wait()
-    for i in range(hrows, rows + 2):
-        if i < rows:
-            normalise(i)
-        if hrows + 1 <= i < rows + 1:
-            weigh(i - 1)
-        if i >= hrows + 2:
-            collect(i - 2)
-    zh_copy.start()
-
-    for q in range(GROUPS):
+
+    def half_add(q):
         half_copy(q).wait_recv()
         for k in range(nk):
             for u in range(gsz):
                 b = own0 + q * gsz + u
-                part[k, b] = (part[k, b].astype(F32) + half_in[k, q * gsz + u].astype(F32)).astype(BF16)
+                part[k, b] = part[k, b] + half_in[k, q * gsz + u]
             rs_copy(k, q, 0).start()
+
+    for i in range(rows + 2):
+        if i < rows and i % gsz == 0:
+            tok_copy(i).wait()
+        if i < rows:
+            normalise(i)
+        if 1 <= i < rows + 1:
+            weigh(i - 1)
+        if i >= 2:
+            collect(i - 2)
+            q, r = divmod(i - 2, 2 * gsz)
+            if r == gsz - 1:
+                if q == 0:
+                    pl.semaphore_wait(barrier, len(greet))
+                half_copy(q).start()
+                if q > 0:
+                    half_add(q - 1)
+    zh_copy.start()
+    half_add(GROUPS - 1)
 
     zh_copy.wait()
     z_part[...] += z_half[...]
@@ -213,17 +213,17 @@
     c_copy = pltpu.make_async_copy(c_v, c_hbm, c_sem)
     c_copy.start()
 
-    def q_copy(k, q, f):
+    def q_copy(k, h, f):
         fu, fv, fc = FLIPS[f]
-        o = ORDERS[q]
+        o = ORDERS[2 * h]
         mu, mv = bits[o[2]], bits[o[3]]
         du = 1 - mu if fu else mu
         dv = 1 - mv if fv else mv
         dc = 1 - core if fc else core
-        i = (k * GROUPS + q) * 7 + f
-        return pltpu.make_async_remote_copy(
-            q_out.at[k, q, dc, du, dv], q_in.at[k, q, core, mu, mv],
-            qs_sem.at[i], qr_sem.at[i], device_id=group_peer(q, f), device_id_type=MESH)
+        i = (k * 2 + h) * 7 + f
+        return pltpu.make_async_remote_copy(
+            q_out.at[k, h, dc, du, dv], q_in.at[k, h, core, mu, mv],
+            qs_sem.at[i], qr_sem.at[i], device_id=group_peer(2 * h, f), device_id_type=MESH)
 
     row8 = lax.broadcasted_iota(jnp.int32, (chip_rows, CHUNK), 0)
     low = row8 < experts
@@ -247,17 +247,23 @@
             rs_copy(k, q, 0).wait()
             for u in range(gsz):
                 at = (k, own0 + q * gsz + u) + region(o, 1)
-                part[at] = (part[at].astype(F32) + r0[k, q * gsz + u].astype(F32)).astype(BF16)
+                part[at] = part[at] + r0[k, q * gsz + u]
             rs_copy(k, q, 1).start()
-    z_copy(0).wait()
-    at = region(ORDERS[0], 1)
-    z_part[at] = z_part[at] + z0[...]
-    z_copy(1).start()
-    for k in range(nk):
-        for q in range(GROUPS):
-            o = ORDERS[q]
-            mu, mv = bits[o[2]], bits[o[3]]
+        if k == 0:
+            z_copy(0).wait()
+            at = region(ORDERS[0], 1)
+            z_part[at] = z_part[at] + z0[...]
+            z_copy(1).start()
+    z_copy(1).wait()
+    at = region(ORDERS[0], 2)
+    z_part[at] = z_part[at] + z1[...]
+    for f in range(3):
+        zq_copy(f).start()
+    for k in range(nk):
+        for q in range(GROUPS):
             rs_copy(k, q, 1).wait()
+        for q in range(GROUPS):
+            h, g = divmod(q, 2)
             for u in range(2):
                 for v in range(2):
                     ev, od = [
@@ -265,16 +271,14 @@
                         + r1[(k, q * gsz + w) + at_recv(q, u, v)].astype(F32)
                         for w in range(gsz)
                     ]
-                    q_out[k, q, 0, u, v] = jnp.where(low, ev, pltpu.roll(od, experts, 0)).astype(BF16)
-                    q_out[k, q, 1, u, v] = jnp.where(low, pltpu.roll(ev, experts, 0), od).astype(BF16)
+                    q_out[k, h, 0, u, v, g] = jnp.where(low, ev, pltpu.roll(od, experts, 0)).astype(BF16)
+                    q_out[k, h, 1, u, v, g] = jnp.where(low, pltpu.roll(ev, experts, 0), od).astype(BF16)
+        for h in range(2):
+            o = ORDERS[2 * h]
+            mu, mv = bits[o[2]], bits[o[3]]
             for f in range(7):
-                q_copy(k, q, f).start()
-            q_in[k, q, core, mu, mv] = q_out[k, q, core, mu, mv]
-    z_copy(1).wait()
-    at = region(ORDERS[0], 2)
-    z_part[at] = z_part[at] + z1[...]
-    for f in range(3):
-        zq_copy(f).start()
+                q_copy(k, h, f).start()
+            q_in[k, h, core, mu, mv] = q_out[k, h, core, mu, mv]
     for f in range(3):
         zq_copy(f).wait()
     z_own = z_part[bits] + (zq[0] + (zq[1] + zq[2]))
@@ -290,13 +294,13 @@
     for cp in wi_copies:
         cp.wait()
     for k in range(nk):
-        for q in range(GROUPS):
+        for h in range(2):
             for f in range(7):
-                q_copy(k, q, f).wait()
+                q_copy(k, h, f).wait()
         for cs in range(2):
             for q in range(GROUPS):
                 p = cs * GROUPS + q
-                s = [q_in[k, q, cs, u, v].astype(F32) for u in range(2) for v in range(2)]
+                s = [q_in[k, q // 2, cs, u, v, q % 2].astype(F32) for u in range(2) for v in range(2)]
                 s = (s[0] + s[1]) + (s[2] + s[3])
                 for t in range(lanes):
                     xs_f[t, p * chip_rows:(p + 1) * chip_rows, :] = s[:, t * 128:(t + 1) * 128]
@@ -310,14 +314,14 @@
     for e in range(experts):
         hid_b[e] = jax.nn.gelu(hid[e], approximate=True).astype(BF16)
 
-    def y_copy(k, q, f):
+    def y_copy(k, h, f):
         _, _, fc = FLIPS[f]
-        o = ORDERS[q]
+        o = ORDERS[2 * h]
         dc = 1 - core if fc else core
-        i = (k * GROUPS + q) * 7 + f
-        return pltpu.make_async_remote_copy(
-            yx.at[k, dc * GROUPS + q], g_in.at[k, q, core, bits[o[2]], bits[o[3]]],
-            ys_sem.at[i], yr_sem.at[i], device_id=group_peer(q, f), device_id_type=MESH)
+        i = (k * 2 + h) * 7 + f
+        return pltpu.make_async_remote_copy(
+            yx.at[k, dc * 2 + h], g_in.at[k, h, core, bits[o[2]], bits[o[3]]],
+            ys_sem.at[i], yr_sem.at[i], device_id=group_peer(2 * h, f), device_id_type=MESH)
 
     def g_copy(k, q, s):
         i = (k * GROUPS + q) * 2 + s
@@ -341,24 +345,26 @@
             for t in range(lanes):
                 ys_f[t, pl.ds(e, rows, stride=experts), :] = ye[:, t * 128:(t + 1) * 128]
         for t in range(lanes):
-            yx[k, :, :, t * 128:(t + 1) * 128] = ys_f[t].reshape(rows // 2, chip_rows, 128).astype(BF16)
-        for q in range(GROUPS):
-            o = ORDERS[q]
+            yx[k, :, :, :, t * 128:(t + 1) * 128] = ys_f[t].reshape(4, 2, chip_rows, 128).astype(BF16)
+        for h in range(2):
+            o = ORDERS[2 * h]
             for f in range(7):
-                y_copy(k, q, f).start()
-            g_in[k, q, core, bits[o[2]], bits[o[3]]] = yx[k, core * GROUPS + q]
-
-    for k in range(nk):
-        for q in range(GROUPS):
+                y_copy(k, h, f).start()
+            g_in[k, h, core, bits[o[2]], bits[o[3]]] = yx[k, core * 2 + h]
+
+    for k in range(nk):
+        for h in range(2):
             for f in range(7):
-                y_copy(k, q, f).wait()
+                y_copy(k, h, f).wait()
+        for q in range(GROUPS):
             for u in range(2):
                 for v in range(2):
-                    s0 = g_in[k, q, 0, u, v].astype(F32)
-                    s1 = g_in[k, q, 1, u, v].astype(F32)
+                    s0 = g_in[k, q // 2, 0, u, v, q % 2].astype(F32)
+                    s1 = g_in[k, q // 2, 1, u, v, q % 2].astype(F32)
                     at = at_rest(q, u, v)
                     gath[(k, own0 + q * gsz) + at] = jnp.where(low, s0, pltpu.roll(s1, experts, 0)).astype(BF16)
                     gath[(k, own0 + q * gsz + 1) + at] = jnp.where(low, pltpu.roll(s0, experts, 0), s1).astype(BF16)
+        for q in range(GROUPS):
             g_copy(k, q, 1).start()
     for k in range(nk):
         for q in range(GROUPS):
@@ -381,7 +387,6 @@
 def _mix_kernel(len_ref, g_hbm, c_hbm, y_hbm, g_v, c_v, y_v, g_sem, c_sem, y_sem):
     rows, tok_count, width = y_v.shape
     nk = g_v.shape[0]
-    nslots = c_v.shape[2]
 
     def c_copy(b):
         return pltpu.make_async_copy(c_hbm.at[b], c_v.at[b], c_sem.at[b])
@@ -396,16 +401,15 @@
         c_copy(b).start()
         g_copy(b).start()
     row_pos = lax.axis_index("seq") * tok_count + lax.broadcasted_iota(jnp.int32, (tok_count, CHUNK), 0)
-    for b0 in range(0, rows, 2):
-        for b in (b0, b0 + 1):
+    for b0 in range(0, rows, 4):
+        for b in range(b0, b0 + 4):
             c_copy(b).wait()
             g_copy(b).wait()
-        for b in (b0, b0 + 1):
+        for b in range(b0, b0 + 4):
             for k in range(nk):
-                gb = g_v[k, b].astype(F32).reshape(nslots, CHUNK).astype(BF16)
-                yk = jnp.where(row_pos < len_ref[b], _nn(c_v[b], gb), 0.0)
+                yk = jnp.where(row_pos < len_ref[b], _nn(c_v[b], g_v[k, b]), 0.0)
                 y_v[b, :, k * CHUNK:(k + 1) * CHUNK] = yk.astype(BF16)
-        for b in (b0, b0 + 1):
+        for b in range(b0, b0 + 4):
             y_copy(b).start()
     for b in range(rows):
         y_copy(b).wait()
@@ -441,8 +445,8 @@
             vm((nk, hrows) + cube + tile, BF16),
             vm((nk, hrows, 2, 2, 2) + tile, BF16),
             vm((nk, hrows, 2, 2) + tile, BF16),
-            vm((nk, GROUPS, 2, 2, 2) + tile, BF16),
-            vm((nk, GROUPS, 2, 2, 2) + tile, BF16),
+            vm((nk, 2, 2, 2, 2, 2) + tile, BF16),
+            vm((nk, 2, 2, 2, 2, 2) + tile, BF16),
             vm(cube + (cr, tok_count), F32),
             vm(cube + (cr, tok_count), F32),
             vm((2, 2, 2, cr, tok_count), F32),
@@ -452,14 +456,14 @@
             vm((experts, rows, ff), F32),
             vm((experts, rows, ff), BF16),
             vm((lanes, rows * experts, 128), F32),
-            vm((nk, rows // 2) + tile, BF16),
-            vm((nk, GROUPS, 2, 2, 2) + tile, BF16),
+            vm((nk, 4, 2) + tile, BF16),
+            vm((nk, 2, 2, 2, 2, 2) + tile, BF16),
             vm(gshape, BF16),
-            dma, dma((2,)), dma((experts,)), dma((experts,)), dma,
+            dma, dma((2 * GROUPS,)), dma((experts,)), dma((experts,)), dma,
             dma((GROUPS,)), dma((GROUPS,)), dma, dma, dma((5,)), dma((5,)),
             dma((nk * GROUPS * 2,)), dma((nk * GROUPS * 2,)),
-            dma((nk * GROUPS * 7,)), dma((nk * GROUPS * 7,)),
-            dma((nk * GROUPS * 7,)), dma((nk * GROUPS * 7,)),
+            dma((nk * 2 * 7,)), dma((nk * 2 * 7,)),
+            dma((nk * 2 * 7,)), dma((nk * 2 * 7,)),
             dma((nk * GROUPS * 2,)), dma((nk * GROUPS * 2,)),
             dma((nk * GROUPS,)), dma((nk * GROUPS,)), dma((nk * GROUPS,)),
         ]
@@ -481,12 +485,12 @@
             in_specs=[smem, anyspace, anyspace],
             out_specs=anyspace,
             scratch_shapes=[
-                vm(gshape, BF16),
+                vm((nk, rows, nslots, CHUNK), BF16),
                 vm((rows, tok_count, nslots), BF16),
                 vm(tok.shape, BF16),
                 dma((rows,)), dma((rows,)), dma((rows,)),
             ],
-        )(lens, gath, comb)
+        )(lens, gath.reshape(nk, rows, nslots, CHUNK), comb)
 
     return jax.shard_map(
         shard_body,

time: 58.8 us -> 56.8 us (0.966)
  Pallas kernels: 57.8 us -> 55.9 us
    pallas_call x1, Pallas kernels: 52.9 us -> 51.1 us  [shard_body(): pl.pallas_call(_exchange_kernel, out_shape=(jax.ShapeDtypeStruct(gshape,...]
where the time goes in v3:
time: 56.8 us; the launch traced here: 56.7 us
  Pallas kernels  55.9 us (98%)
  between operations  0.82 us (1%)
    pallas_call x1, Pallas kernels, shard_body(): pl.pallas_call(_exchange_kernel, out_shape=(jax.ShapeDtypeStruct(gshape,...  51.1 us
    pallas_call x1, Pallas kernels, shard_body(): pl.pallas_call(_mix_kernel, out_shape=jax.ShapeDtypeStruct(tok.shape, BF1...  4.71 us

profile of v3, /device:TPU:97, one launch (start us, length us, event | category | flops | bytes accessed | tf_op | source)
XLA Modules:
  0.0 56.7 jit_solution(14582863030541885620)
XLA Ops:
  0.7 51.1 %shard_map.64 = (bf16[3,16,2,2,2,2,8,256]{7,6,5,4,3,2,1,0:T(8,128)(2,1)}, bf16[16,128,128]{2,1,0:T(8,128)(2,1)}) custom-call(s32[16]{0:T(128)} %len_ref.3, f32[1]{0:T(128)S(6)} %copy.7.gain_ref, bf16[16,128,768]{2,1,0:T(8,128)(2,1)} %tok_hbm.1, bf16[768,128]{1,0:T(8,128)(2,1)} %phi_hbm.1, bf16[4,768,3072]{2,1,0:T(8,128)(2,1)} %wi_hbm.1, ...), custom_call_target="tpu_custom_call" | custom-call | tf_op jit(solution)/shard_map/pallas_call | solution.py:470
  51.8 4.7 %shard_map.65 = bf16[16,128,768]{2,1,0:T(8,128)(2,1)} custom-call(s32[16]{0:T(128)} %len_ref.3, bf16[3,16,128,256]{3,2,1,0:T(8,128)(2,1)} %bitcast.1, bf16[16,128,128]{2,1,0:T(8,128)(2,1)} %get-tuple-element.8.c_hbm), custom_call_target="tpu_custom_call" | custom-call | tf_op jit(solution)/shard_map/pallas_call | solution.py:482

commit v4 on v3

--- a/solution.py
+++ b/solution.py
@@ -22,6 +22,10 @@
 
 def _nn(a, b):
     return jnp.dot(a, b, preferred_element_type=F32)
+
+
+def _drain(ref, sem):
+    pltpu.make_async_copy(ref, ref, sem).wait()
 
 
 def _exchange_kernel(len_ref, gain_ref, tok_hbm, phi_hbm, wi_hbm, wo_hbm, g_hbm, c_hbm,
@@ -75,18 +79,19 @@
         pl.semaphore_signal(barrier, inc=1, device_id=d, device_id_type=MESH)
 
     def batch(i):
-        q, r = divmod(i, 2 * gsz)
-        return (oth0 if r < gsz else own0 - gsz) + q * gsz + r
+        return oth0 + i if i < hrows else own0 + i - hrows
+
+    tok_step = rows // 4
 
     def tok_copy(i):
-        at = pl.ds(batch(i), gsz)
-        return pltpu.make_async_copy(tok_hbm.at[at], x_v.at[at], tok_sem.at[i // gsz])
+        at = pl.ds(batch(i), tok_step)
+        return pltpu.make_async_copy(tok_hbm.at[at], x_v.at[at], tok_sem.at[i // tok_step])
 
     phi_copy = pltpu.make_async_copy(phi_hbm, phi_v, phi_sem)
-    wi_copies = [pltpu.make_async_copy(wi_hbm.at[e], wi_v.at[e], wi_sem.at[e]) for e in range(experts)]
-    wo_copies = [pltpu.make_async_copy(wo_hbm.at[e], wo_v.at[e], wo_sem.at[e]) for e in range(experts)]
+    wi_copies = [pltpu.make_async_copy(wi_hbm.at[e], wi_v.at[e], wi_sem) for e in range(experts)]
+    wo_copies = [pltpu.make_async_copy(wo_hbm.at[e], wo_v.at[e], wo_sem) for e in range(experts)]
     phi_copy.start()
-    for i in range(0, rows, gsz):
+    for i in range(0, rows, tok_step):
         tok_copy(i).start()
 
     z_part[...] = jnp.zeros_like(z_part)
@@ -117,7 +122,7 @@
     def half_copy(q):
         return pltpu.make_async_remote_copy(
             part.at[:, pl.ds(oth0 + q * gsz, gsz)], half_in.at[:, pl.ds(q * gsz, gsz)],
-            hs_sem.at[q], hr_sem.at[q], device_id=mate, device_id_type=MESH)
+            hs_sem, hr_sem.at[q], device_id=mate, device_id_type=MESH)
 
     def region(order, fixed, flip=None):
         idx = [slice(None)] * 4
@@ -132,11 +137,10 @@
 
     def rs_copy(k, q, s):
         order = ORDERS[q]
-        i = (k * GROUPS + q) * 2 + s
         return pltpu.make_async_remote_copy(
             part.at[(k, pl.ds(own0 + q * gsz, gsz)) + region(order, s, order[s])],
             rbuf[s].at[k, pl.ds(q * gsz, gsz)],
-            rs_sem.at[i], rr_sem.at[i], device_id=steps[order[s]], device_id_type=MESH)
+            rs_sem.at[s], rr_sem.at[2 * k + s], device_id=steps[order[s]], device_id_type=MESH)
 
     def z_copy(s):
         order = ORDERS[0]
@@ -152,12 +156,16 @@
             if on:
                 idx[d] = 1 - idx[d]
         return pltpu.make_async_remote_copy(
-            z_part.at[tuple(idx)], zq.at[f], zs_sem.at[2 + f], zr_sem.at[2 + f],
+            z_part.at[tuple(idx)], zq.at[f], zs_sem.at[2], zr_sem.at[2],
             device_id=group_peer(0, f), device_id_type=MESH)
 
     zh_copy = pltpu.make_async_remote_copy(
         z_part, z_half, zhs_sem, zhr_sem, device_id=mate, device_id_type=MESH)
 
+    ahead = 4
+    tok_copy(0).wait()
+    for i in range(ahead):
+        normalise(i)
     phi_copy.wait()
     pf = phi_v[...].astype(F32)
     pn = (pf * (gain * lax.rsqrt(jnp.sum(pf * pf, axis=0, keepdims=True) + 1e-6))).astype(BF16)
@@ -180,24 +188,25 @@
                 part[k, b] = part[k, b] + half_in[k, q * gsz + u]
             rs_copy(k, q, 0).start()
 
-    for i in range(rows + 2):
-        if i < rows and i % gsz == 0:
-            tok_copy(i).wait()
+    for i in range(rows + 1):
+        if i + ahead < rows:
+            if (i + ahead) % tok_step == 0:
+                tok_copy(i + ahead).wait()
+            normalise(i + ahead)
         if i < rows:
-            normalise(i)
-        if 1 <= i < rows + 1:
-            weigh(i - 1)
-        if i >= 2:
-            collect(i - 2)
-            q, r = divmod(i - 2, 2 * gsz)
+            weigh(i)
+        if i == rows - 1:
+            zh_copy.start()
+        if i >= 1:
+            collect(i - 1)
+            q, r = divmod(i - 1, gsz)
             if r == gsz - 1:
                 if q == 0:
                     pl.semaphore_wait(barrier, len(greet))
-                half_copy(q).start()
-                if q > 0:
-                    half_add(q - 1)
-    zh_copy.start()
-    half_add(GROUPS - 1)
+                if q < GROUPS:
+                    half_copy(q).start()
+                else:
+                    half_add(q - GROUPS)
 
     zh_copy.wait()
     z_part[...] += z_half[...]
@@ -220,10 +229,9 @@
         du = 1 - mu if fu else mu
         dv = 1 - mv if fv else mv
         dc = 1 - core if fc else core
-        i = (k * 2 + h) * 7 + f
-        return pltpu.make_async_remote_copy(
-            q_out.at[k, h, dc, du, dv], q_in.at[k, h, core, mu, mv],
-            qs_sem.at[i], qr_sem.at[i], device_id=group_peer(2 * h, f), device_id_type=MESH)
+        return pltpu.make_async_remote_copy(
+            q_out.at[k, h, dc, du, dv], q_in.at[k, 4 * core + 2 * mu + mv, h],
+            qs_sem, qr_sem.at[k], device_id=group_peer(2 * h, f), device_id_type=MESH)
 
     row8 = lax.broadcasted_iota(jnp.int32, (chip_rows, CHUNK), 0)
     low = row8 < experts
@@ -242,26 +250,24 @@
         return tuple(val[d] for d in free)
 
     for k in range(nk):
-        for q in range(GROUPS):
-            o = ORDERS[q]
-            rs_copy(k, q, 0).wait()
+        _drain(r0.at[k], rr_sem.at[2 * k])
+        for q in range(GROUPS):
             for u in range(gsz):
-                at = (k, own0 + q * gsz + u) + region(o, 1)
+                at = (k, own0 + q * gsz + u) + region(ORDERS[q], 1)
                 part[at] = part[at] + r0[k, q * gsz + u]
             rs_copy(k, q, 1).start()
         if k == 0:
-            z_copy(0).wait()
+            z_copy(0).wait_recv()
             at = region(ORDERS[0], 1)
             z_part[at] = z_part[at] + z0[...]
             z_copy(1).start()
-    z_copy(1).wait()
+    z_copy(1).wait_recv()
     at = region(ORDERS[0], 2)
     z_part[at] = z_part[at] + z1[...]
     for f in range(3):
         zq_copy(f).start()
     for k in range(nk):
-        for q in range(GROUPS):
-            rs_copy(k, q, 1).wait()
+        _drain(r1.at[k], rr_sem.at[2 * k + 1])
         for q in range(GROUPS):
             h, g = divmod(q, 2)
             for u in range(2):
@@ -278,9 +284,8 @@
             mu, mv = bits[o[2]], bits[o[3]]
             for f in range(7):
                 q_copy(k, h, f).start()
-            q_in[k, h, core, mu, mv] = q_out[k, h, core, mu, mv]
-    for f in range(3):
-        zq_copy(f).wait()
+            q_in[k, 4 * core + 2 * mu + mv, h] = q_out[k, h, core, mu, mv]
+    _drain(zq, zr_sem.at[2])
     z_own = z_part[bits] + (zq[0] + (zq[1] + zq[2]))
     zrow = lax.broadcasted_iota(jnp.int32, z_own.shape, 0)
     eye = lax.broadcasted_iota(jnp.int32, (rows, z_own.shape[1]), 0) == lax.broadcasted_iota(
@@ -291,16 +296,13 @@
         z_inv.append(1.0 / jnp.sum(jnp.where(eye, zr, 0.0), axis=1, keepdims=True))
 
     lanes = CHUNK // 128
-    for cp in wi_copies:
-        cp.wait()
-    for k in range(nk):
-        for h in range(2):
-            for f in range(7):
-                q_copy(k, h, f).wait()
+    _drain(wi_v, wi_sem)
+    for k in range(nk):
+        _drain(q_in.at[k, pl.ds(0, 7)], qr_sem.at[k])
         for cs in range(2):
             for q in range(GROUPS):
                 p = cs * GROUPS + q
-                s = [q_in[k, q // 2, cs, u, v, q % 2].astype(F32) for u in range(2) for v in range(2)]
+                s = [q_in[k, 4 * cs + j, q // 2, q % 2].astype(F32) for j in range(4)]
                 s = (s[0] + s[1]) + (s[2] + s[3])
                 for t in range(lanes):
                     xs_f[t, p * chip_rows:(p + 1) * chip_rows, :] = s[:, t * 128:(t + 1) * 128]
@@ -309,8 +311,7 @@
             xe = jnp.concatenate([xs_f[t, pick, :] for t in range(lanes)], axis=1)
             h = _nn((xe * z_inv[e]).astype(BF16), wi_v[e, k * CHUNK:(k + 1) * CHUNK, :])
             hid[e] = h if k == 0 else hid[e] + h
-    for cp in wo_copies:
-        cp.wait()
+    _drain(wo_v, wo_sem)
     for e in range(experts):
         hid_b[e] = jax.nn.gelu(hid[e], approximate=True).astype(BF16)
 
@@ -318,26 +319,23 @@
         _, _, fc = FLIPS[f]
         o = ORDERS[2 * h]
         dc = 1 - core if fc else core
-        i = (k * 2 + h) * 7 + f
-        return pltpu.make_async_remote_copy(
-            yx.at[k, dc * 2 + h], g_in.at[k, h, core, bits[o[2]], bits[o[3]]],
-            ys_sem.at[i], yr_sem.at[i], device_id=group_peer(2 * h, f), device_id_type=MESH)
+        return pltpu.make_async_remote_copy(
+            yx.at[k, dc * 2 + h], g_in.at[k, 4 * core + 2 * bits[o[2]] + bits[o[3]], h],
+            ys_sem, yr_sem.at[k], device_id=group_peer(2 * h, f), device_id_type=MESH)
 
     def g_copy(k, q, s):
-        i = (k * GROUPS + q) * 2 + s
         ref = gath.at[(k, pl.ds(own0 + q * gsz, gsz)) + region(ORDERS[q], s + 1)]
         return pltpu.make_async_remote_copy(
-            ref, ref, gs_sem.at[i], gr_sem.at[i], device_id=steps[ORDERS[q][s]], device_id_type=MESH)
+            ref, ref, gs_sem.at[s], gr_sem.at[2 * k + s], device_id=steps[ORDERS[q][s]], device_id_type=MESH)
 
     def gd_copy(k, q):
         at = (k, pl.ds(own0 + q * gsz, gsz))
-        i = k * GROUPS + q
-        return pltpu.make_async_remote_copy(
-            gath.at[at], g_hbm.at[at], gds_sem.at[i], gdr_sem.at[i], device_id=mate, device_id_type=MESH)
+        return pltpu.make_async_remote_copy(
+            gath.at[at], g_hbm.at[at], gds_sem, gdr_sem, device_id=mate, device_id_type=MESH)
 
     def go_copy(k, q):
         at = (k, pl.ds(own0 + q * gsz, gsz))
-        return pltpu.make_async_copy(gath.at[at], g_hbm.at[at], go_sem.at[k * GROUPS + q])
+        return pltpu.make_async_copy(gath.at[at], g_hbm.at[at], go_sem)
 
     for k in range(nk):
         for e in range(experts):
@@ -350,37 +348,42 @@
             o = ORDERS[2 * h]
             for f in range(7):
                 y_copy(k, h, f).start()
-            g_in[k, h, core, bits[o[2]], bits[o[3]]] = yx[k, core * 2 + h]
-
-    for k in range(nk):
-        for h in range(2):
-            for f in range(7):
-                y_copy(k, h, f).wait()
+            g_in[k, 4 * core + 2 * bits[o[2]] + bits[o[3]], h] = yx[k, core * 2 + h]
+
+    for k in range(nk):
+        _drain(g_in.at[k, pl.ds(0, 7)], yr_sem.at[k])
         for q in range(GROUPS):
             for u in range(2):
                 for v in range(2):
-                    s0 = g_in[k, q // 2, 0, u, v, q % 2].astype(F32)
-                    s1 = g_in[k, q // 2, 1, u, v, q % 2].astype(F32)
+                    s0 = g_in[k, 2 * u + v, q // 2, q % 2].astype(F32)
+                    s1 = g_in[k, 4 + 2 * u + v, q // 2, q % 2].astype(F32)
                     at = at_rest(q, u, v)
                     gath[(k, own0 + q * gsz) + at] = jnp.where(low, s0, pltpu.roll(s1, experts, 0)).astype(BF16)
                     gath[(k, own0 + q * gsz + 1) + at] = jnp.where(low, pltpu.roll(s0, experts, 0), s1).astype(BF16)
         for q in range(GROUPS):
             g_copy(k, q, 1).start()
     for k in range(nk):
-        for q in range(GROUPS):
-            g_copy(k, q, 1).wait()
+        _drain(r1.at[k], gr_sem.at[2 * k + 1])
+        for q in range(GROUPS):
             g_copy(k, q, 0).start()
     for k in range(nk):
-        for q in range(GROUPS):
-            g_copy(k, q, 0).wait()
+        _drain(r0.at[k], gr_sem.at[2 * k])
+        for q in range(GROUPS):
             gd_copy(k, q).start()
             go_copy(k, q).start()
-    for k in range(nk):
-        for q in range(GROUPS):
-            gd_copy(k, q).wait()
-            go_copy(k, q).wait()
-    for q in range(GROUPS):
-        half_copy(q).wait_send()
+    z_copy(0).wait_send()
+    z_copy(1).wait_send()
+    _drain(half_in, hs_sem)
+    _drain(zq, zs_sem.at[2])
+    _drain(r0, rs_sem.at[0])
+    _drain(r1, rs_sem.at[1])
+    _drain(q_in.at[:, pl.ds(0, 7)], qs_sem)
+    _drain(g_in.at[:, pl.ds(0, 7)], ys_sem)
+    _drain(r0, gs_sem.at[0])
+    _drain(r1, gs_sem.at[1])
+    _drain(half_in, gds_sem)
+    _drain(half_in, go_sem)
+    _drain(half_in, gdr_sem)
     c_copy.wait()
 
 
@@ -388,31 +391,30 @@
     rows, tok_count, width = y_v.shape
     nk = g_v.shape[0]
 
-    def c_copy(b):
-        return pltpu.make_async_copy(c_hbm.at[b], c_v.at[b], c_sem.at[b])
+    step = rows // 4
 
     def g_copy(b):
-        return pltpu.make_async_copy(g_hbm.at[:, b], g_v.at[:, b], g_sem.at[b])
+        at = pl.ds(b, step)
+        return pltpu.make_async_copy(g_hbm.at[:, at], g_v.at[:, at], g_sem.at[b // step])
 
     def y_copy(b):
-        return pltpu.make_async_copy(y_v.at[b], y_hbm.at[b], y_sem.at[b])
-
-    for b in range(rows):
-        c_copy(b).start()
+        at = pl.ds(b, step)
+        return pltpu.make_async_copy(y_v.at[at], y_hbm.at[at], y_sem)
+
+    c_copy = pltpu.make_async_copy(c_hbm, c_v, c_sem)
+    c_copy.start()
+    for b in range(0, rows, step):
         g_copy(b).start()
     row_pos = lax.axis_index("seq") * tok_count + lax.broadcasted_iota(jnp.int32, (tok_count, CHUNK), 0)
-    for b0 in range(0, rows, 4):
-        for b in range(b0, b0 + 4):
-            c_copy(b).wait()
-            g_copy(b).wait()
-        for b in range(b0, b0 + 4):
+    c_copy.wait()
+    for b0 in range(0, rows, step):
+        g_copy(b0).wait()
+        for b in range(b0, b0 + step):
             for k in range(nk):
                 yk = jnp.where(row_pos < len_ref[b], _nn(c_v[b], g_v[k, b]), 0.0)
                 y_v[b, :, k * CHUNK:(k + 1) * CHUNK] = yk.astype(BF16)
-        for b in range(b0, b0 + 4):
-            y_copy(b).start()
-    for b in range(rows):
-        y_copy(b).wait()
+        y_copy(b0).start()
+    _drain(y_v, y_sem)
 
 
 def solution(mesh):
@@ -446,7 +448,7 @@
             vm((nk, hrows, 2, 2, 2) + tile, BF16),
             vm((nk, hrows, 2, 2) + tile, BF16),
             vm((nk, 2, 2, 2, 2, 2) + tile, BF16),
-            vm((nk, 2, 2, 2, 2, 2) + tile, BF16),
+            vm((nk, 8, 2, 2) + tile, BF16),
             vm(cube + (cr, tok_count), F32),
             vm(cube + (cr, tok_count), F32),
             vm((2, 2, 2, cr, tok_count), F32),
@@ -457,15 +459,11 @@
             vm((experts, rows, ff), BF16),
             vm((lanes, rows * experts, 128), F32),
             vm((nk, 4, 2) + tile, BF16),
-            vm((nk, 2, 2, 2, 2, 2) + tile, BF16),
+            vm((nk, 8, 2, 2) + tile, BF16),
             vm(gshape, BF16),
-            dma, dma((2 * GROUPS,)), dma((experts,)), dma((experts,)), dma,
-            dma((GROUPS,)), dma((GROUPS,)), dma, dma, dma((5,)), dma((5,)),
-            dma((nk * GROUPS * 2,)), dma((nk * GROUPS * 2,)),
-            dma((nk * 2 * 7,)), dma((nk * 2 * 7,)),
-            dma((nk * 2 * 7,)), dma((nk * 2 * 7,)),
-            dma((nk * GROUPS * 2,)), dma((nk * GROUPS * 2,)),
-            dma((nk * GROUPS,)), dma((nk * GROUPS,)), dma((nk * GROUPS,)),
+            dma, dma((4,)), dma, dma, dma,
+            dma, dma((GROUPS,)), dma, dma, dma((3,)), dma((3,)), dma((2,)), dma((2 * nk,)),
+            dma, dma((nk,)), dma, dma((nk,)), dma((2,)), dma((2 * nk,)), dma, dma, dma,
         ]
         gath, comb = pl.pallas_call(
             _exchange_kernel,
@@ -488,7 +486,7 @@
                 vm((nk, rows, nslots, CHUNK), BF16),
                 vm((rows, tok_count, nslots), BF16),
                 vm(tok.shape, BF16),
-                dma((rows,)), dma((rows,)), dma((rows,)),
+                dma((4,)), dma, dma,
             ],
         )(lens, gath.reshape(nk, rows, nslots, CHUNK), comb)
 

time: 56.8 us -> 53.2 us (0.937)
  Pallas kernels: 55.9 us -> 52.3 us
    pallas_call x1, Pallas kernels: 51.1 us -> 47.5 us  [shard_body(): pl.pallas_call(_exchange_kernel, out_shape=(jax.ShapeDtypeStruct(gshape,...]
where the time goes in v4:
time: 53.2 us; the launch traced here: 53.1 us
  Pallas kernels  52.3 us (98%)
  between operations  0.82 us (2%)
    pallas_call x1, Pallas kernels, shard_body(): pl.pallas_call(_exchange_kernel, out_shape=(jax.ShapeDtypeStruct(gshape,...  47.5 us
    pallas_call x1, Pallas kernels, shard_body(): pl.pallas_call(_mix_kernel, out_shape=jax.ShapeDtypeStruct(tok.shape, BF1...  4.77 us

profile of v4, /device:TPU:97, one launch (start us, length us, event | category | flops | bytes accessed | tf_op | source)
XLA Modules:
  0.0 53.1 jit_solution(7143859676647166079)
XLA Ops:
  0.7 47.5 %shard_map.64 = (bf16[3,16,2,2,2,2,8,256]{7,6,5,4,3,2,1,0:T(8,128)(2,1)}, bf16[16,128,128]{2,1,0:T(8,128)(2,1)}) custom-call(s32[16]{0:T(128)} %len_ref.3, f32[1]{0:T(128)S(6)} %copy.7.gain_ref, bf16[16,128,768]{2,1,0:T(8,128)(2,1)} %tok_hbm.1, bf16[768,128]{1,0:T(8,128)(2,1)} %phi_hbm.1, bf16[4,768,3072]{2,1,0:T(8,128)(2,1)} %wi_hbm.1, ...), custom_call_target="tpu_custom_call" | custom-call | tf_op jit(solution)/shard_map/pallas_call | solution.py:468
  48.2 4.8 %shard_map.65 = bf16[16,128,768]{2,1,0:T(8,128)(2,1)} custom-call(s32[16]{0:T(128)} %len_ref.3, bf16[3,16,128,256]{3,2,1,0:T(8,128)(2,1)} %bitcast.1, bf16[16,128,128]{2,1,0:T(8,128)(2,1)} %get-tuple-element.8.c_hbm), custom_call_target="tpu_custom_call" | custom-call | tf_op jit(solution)/shard_map/pallas_call | solution.py:480

commit v5 on v4

v5 whole, which is shorter than its diff:
```python
import functools

import jax
import jax.numpy as jnp
from jax import lax
from jax.experimental import pallas as pl
from jax.experimental.pallas import tpu as pltpu
from jax.sharding import PartitionSpec as P

WIDE = 256
WIDTHS = (256, 256, 128, 128)
OFFS = tuple(sum(WIDTHS[:k]) for k in range(len(WIDTHS)))
NK = len(WIDTHS)
GROUPS = 4
F32 = jnp.float32
BF16 = jnp.bfloat16
MESH = pl.DeviceIdType.MESH
ORDERS = ((3, 1, 2, 0), (1, 3, 2, 0), (2, 0, 3, 1), (0, 2, 3, 1))
FLIPS = tuple((f & 1, (f >> 1) & 1, (f >> 2) & 1) for f in range(1, 8))


def _nt(a, b):
    return lax.dot_general(a, b, (((1,), (1,)), ((), ())), preferred_element_type=F32)


def _nn(a, b):
    return jnp.dot(a, b, preferred_element_type=F32)


def _drain(ref, sem):
    pltpu.make_async_copy(ref, ref, sem).wait()


def _exchange_kernel(*refs):
    it = iter(refs)

    def take(n=NK):
        return [next(it) for _ in range(n)]

    len_ref, gain_ref, tok_hbm, phi_hbm, wi_hbm, wo_hbm = take(6)
    g_hbm = take()
    c_hbm = next(it)
    x_v, xn_v, w_v, phi_v, phit_v, wi_v, wo_v, ct_v, c_v = take(9)
    part, half_in, r0, r1, q_out, q_in, yx, g_in, gath = [take() for _ in range(9)]
    z_part, z_half, z0, z1, zq, xs_f, hid, hid_b, ys_f = take(9)
    (phi_sem, tok_sem, wi_sem, wo_sem, c_sem, hs_sem, hr_sem, zhs_sem, zhr_sem, zs_sem, zr_sem,
     rs_sem, rr_sem, qs_sem, qr_sem, ys_sem, yr_sem, gs_sem, gr_sem, gds_sem, gdr_sem, go_sem) = take(22)
    rows, tok_count, width = x_v.shape
    experts = wi_v.shape[0]
    hrows = rows // 2
    gsz = hrows // GROUPS
    nslots = phit_v.shape[0]
    chip_rows = 2 * experts
    chunks = tuple(zip(range(NK), OFFS, WIDTHS))
    me = lax.axis_index("seq")
    core = lax.rem(me, 2)
    chip = me // 2
    x = lax.rem(chip, 4)
    y = chip // 4
    xb = x // 2
    xa = lax.rem(x + xb, 2)
    yb = y // 2
    ya = lax.rem(y + yb, 2)
    bits = (yb, ya, xb, xa)

    def peer(dims, flip_core=0):
        b = [1 - v if d in dims else v for d, v in enumerate(bits)]
        yy = 2 * b[0] + lax.rem(b[0] + b[1], 2)
        xx = 2 * b[2] + lax.rem(b[2] + b[3], 2)
        return {"seq": (yy * 4 + xx) * 2 + (1 - core if flip_core else core)}

    def group_peer(q, f):
        fu, fv, fc = FLIPS[f]
        dims = tuple(d for d, on in zip(ORDERS[q][2:], (fu, fv)) if on)
        return peer(dims, fc)

    mate = peer((), 1)
    steps = tuple(peer((d,)) for d in range(4))
    own0 = core * hrows
    oth0 = (1 - core) * hrows

    tok_step = rows // 4

    def batch(i):
        return oth0 + i if i < hrows else own0 + i - hrows

    def tok_copy(i):
        at = pl.ds(batch(i), tok_step)
        return pltpu.make_async_copy(tok_hbm.at[at], x_v.at[at], tok_sem.at[i // tok_step])

    phi_copy = pltpu.make_async_copy(phi_hbm, phi_v, phi_sem)
    wi_copies = [pltpu.make_async_copy(wi_hbm.at[e], wi_v.at[e], wi_sem) for e in range(experts)]
    wo_copies = [pltpu.make_async_copy(wo_hbm.at[e], wo_v.at[e], wo_sem) for e in range(experts)]
    tok_copy(0).start()
    phi_copy.start()
    tok_copy(tok_step).start()

    pairs = sorted({tuple(sorted(o[2:])) for o in ORDERS})
    greet = [mate]
    for fc in (0, 1):
        greet += [peer((d,), fc) for d in range(4)]
        greet += [peer(dims, fc) for dims in pairs]
    barrier = pltpu.get_barrier_semaphore()
    for d in greet:
        pl.semaphore_signal(barrier, inc=1, device_id=d, device_id_type=MESH)

    z_part[...] = jnp.zeros_like(z_part)
    gain = gain_ref[0]
    shift = gain * (1.0 + 2.0 ** -7)
    lane = lax.broadcasted_iota(jnp.int32, (nslots, tok_count), 1)
    pos = me * tok_count + lane

    def normalise(i):
        xf = x_v[batch(i)].astype(F32)
        xn_v[i] = (xf * lax.rsqrt(jnp.sum(xf * xf, axis=1, keepdims=True) + 1e-6)).astype(BF16)

    def weigh(i):
        b = batch(i)
        ex = jnp.exp(_nt(phit_v[...], xn_v[i]) - shift)
        ct_v[b] = (ex * (1.0 / jnp.sum(ex, axis=0, keepdims=True))).astype(BF16)
        exm = jnp.where(pos < len_ref[b], ex, 0.0)
        w_v[i] = exm.astype(BF16)
        zs = jnp.where(lane == b, jnp.sum(exm, axis=1, keepdims=True), 0.0)
        z_part[...] += zs.reshape(z_part.shape)

    def collect(i):
        b = batch(i)
        for base in range(0, width, WIDE):
            pk = _nn(w_v[i], x_v[b, :, base:base + WIDE])
            for k, off, wd in chunks:
                if base <= off < base + WIDE:
                    piece = pk[:, off - base:off - base + wd]
                    part[k][b] = piece.reshape(2, 2, 2, 2, chip_rows, wd).astype(BF16)

    def half_copy(k, h):
        n = hrows // 2
        return pltpu.make_async_remote_copy(
            part[k].at[pl.ds(oth0 + h * n, n)], half_in[k].at[pl.ds(h * n, n)],
            hs_sem, hr_sem.at[k], device_id=mate, device_id_type=MESH)

    def region(order, fixed, flip=None):
        idx = [slice(None)] * 4
        for t in range(fixed):
            idx[order[t]] = bits[order[t]]
        if flip is not None:
            idx[flip] = 1 - bits[flip]
        return tuple(idx)

    rbuf = (r0, r1)
    zbuf = (z0, z1)

    def rs_copy(k, q, s):
        order = ORDERS[q]
        return pltpu.make_async_remote_copy(
            part[k].at[(pl.ds(own0 + q * gsz, gsz),) + region(order, s, order[s])],
            rbuf[s][k].at[pl.ds(q * gsz, gsz)],
            rs_sem.at[s], rr_sem.at[2 * k + s], device_id=steps[order[s]], device_id_type=MESH)

    def z_copy(s):
        order = ORDERS[0]
        return pltpu.make_async_remote_copy(
            z_part.at[region(order, s, order[s])], zbuf[s],
            zs_sem.at[s], zr_sem.at[s], device_id=steps[order[s]], device_id_type=MESH)

    def zq_copy(f):
        fu, fv, _ = FLIPS[f]
        order = ORDERS[0]
        idx = list(bits)
        for d, on in zip(order[2:], (fu, fv)):
            if on:
                idx[d] = 1 - idx[d]
        return pltpu.make_async_remote_copy(
            z_part.at[tuple(idx)], zq.at[f], zs_sem.at[2], zr_sem.at[2],
            device_id=group_peer(0, f), device_id_type=MESH)

    zh_copy = pltpu.make_async_remote_copy(
        z_part, z_half, zhs_sem, zhr_sem, device_id=mate, device_id_type=MESH)

    tok_copy(0).wait()
    tok_copy(2 * tok_step).start()
    tok_copy(3 * tok_step).start()
    for i in range(tok_step):
        normalise(i)
    phi_copy.wait()
    pf = phi_v[...].astype(F32)
    pn = (pf * (gain * lax.rsqrt(jnp.sum(pf * pf, axis=0, keepdims=True) + 1e-6))).astype(BF16)
    new = lax.broadcasted_iota(jnp.int32, (nslots, nslots), 0)
    old = lax.broadcasted_iota(jnp.int32, (nslots, nslots), 1)
    nchip = new // chip_rows
    nxa, nxb, nya, nyb = nchip & 1, (nchip >> 1) & 1, (nchip >> 2) & 1, (nchip >> 3) & 1
    src = ((2 * nyb + (nya ^ nyb)) * 4 + 2 * nxb + (nxa ^ nxb)) * chip_rows + (new & (chip_rows - 1))
    perm = jnp.where(src == old, 1.0, 0.0).astype(BF16)
    phit_v[...] = _nt(perm, pn).astype(BF16)
    for cp in wi_copies + wo_copies:
        cp.start()

    def front(lo, hi, norm):
        norm = iter(norm)
        for i in range(lo, hi + 1):
            if i < hi:
                weigh(i)
            j = next(norm, None)
            if j is not None:
                normalise(j)
            if i > lo:
                collect(i - 1)

    tok_copy(tok_step).wait()
    front(0, tok_step, range(tok_step, 2 * tok_step))
    pl.semaphore_wait(barrier, len(greet))
    for k in range(NK):
        half_copy(k, 0).start()
    tok_copy(2 * tok_step).wait()
    front(tok_step, 2 * tok_step, range(2 * tok_step, 3 * tok_step))
    for k in range(NK):
        half_copy(k, 1).start()
    tok_copy(3 * tok_step).wait()
    front(2 * tok_step, rows, range(3 * tok_step, rows))
    zh_copy.start()

    for k in range(NK):
        _drain(half_in[k], hr_sem.at[k])
        for j in range(hrows):
            part[k][own0 + j] = part[k][own0 + j] + half_in[k][j]
        for q in range(GROUPS):
            rs_copy(k, q, 0).start()

    zh_copy.wait()
    z_part[...] += z_half[...]
    z_copy(0).start()


    def flip_c(i, carry):
        for u in range(4):
            c_v[4 * i + u] = ct_v[4 * i + u].astype(F32).T.astype(BF16)
        return carry

    lax.fori_loop(0, rows // 4, flip_c, 0)
    c_copy = pltpu.make_async_copy(c_v, c_hbm, c_sem)
    c_copy.start()

    def src_at(h):
        o = ORDERS[2 * h]
        return 4 * core + 2 * bits[o[2]] + bits[o[3]]

    def dst_at(h, f):
        fu, fv, fc = FLIPS[f]
        o = ORDERS[2 * h]
        mu, mv = bits[o[2]], bits[o[3]]
        return (1 - core if fc else core), (1 - mu if fu else mu), (1 - mv if fv else mv)

    def q_copy(k, h, f):
        dc, du, dv = dst_at(h, f)
        return pltpu.make_async_remote_copy(
            q_out[k].at[h, 4 * dc + 2 * du + dv], q_in[k].at[src_at(h), h],
            qs_sem, qr_sem.at[k], device_id=group_peer(2 * h, f), device_id_type=MESH)

    def low(wd):
        return lax.broadcasted_iota(jnp.int32, (chip_rows, wd), 0) < experts

    def at_rest(q, u, v):
        o = ORDERS[q]
        idx = list(bits)
        idx[o[2]] = u
        idx[o[3]] = v
        return tuple(idx)

    def at_recv(q, u, v):
        o = ORDERS[q]
        free = sorted(o[2:])
        val = {o[2]: u, o[3]: v}
        return tuple(val[d] for d in free)

    for k in range(NK):
        _drain(r0[k], rr_sem.at[2 * k])
        for q in range(GROUPS):
            for u in range(gsz):
                at = (own0 + q * gsz + u,) + region(ORDERS[q], 1)
                part[k][at] = part[k][at] + r0[k][q * gsz + u]
            rs_copy(k, q, 1).start()
        if k == 0:
            z_copy(0).wait_recv()
            at = region(ORDERS[0], 1)
            z_part[at] = z_part[at] + z0[...]
            z_copy(1).start()

    for k, _, wd in chunks:
        _drain(r1[k], rr_sem.at[2 * k + 1])
        for q in range(GROUPS):
            h, g = divmod(q, 2)
            for u in range(2):
                for v in range(2):
                    ev, od = [
                        part[k][(own0 + q * gsz + w,) + at_rest(q, u, v)].astype(F32)
                        + r1[k][(q * gsz + w,) + at_recv(q, u, v)].astype(F32)
                        for w in range(gsz)
                    ]
                    d = 2 * u + v
                    q_out[k][h, d, g] = jnp.where(low(wd), ev, pltpu.roll(od, experts, 0)).astype(BF16)
                    q_out[k][h, 4 + d, g] = jnp.where(low(wd), pltpu.roll(ev, experts, 0), od).astype(BF16)
        for h in range(2):
            for f in range(7):
                q_copy(k, h, f).start()
            q_in[k][src_at(h), h] = q_out[k][h, src_at(h)]
        if k == 0:
            z_copy(1).wait_recv()
            at = region(ORDERS[0], 2)
            z_part[at] = z_part[at] + z1[...]
            for f in range(3):
                zq_copy(f).start()
    _drain(zq, zr_sem.at[2])
    z_own = z_part[bits] + (zq[0] + (zq[1] + zq[2]))
    zrow = lax.broadcasted_iota(jnp.int32, z_own.shape, 0)
    eye = lax.broadcasted_iota(jnp.int32, (rows, z_own.shape[1]), 0) == lax.broadcasted_iota(
        jnp.int32, (rows, z_own.shape[1]), 1)
    z_inv = []
    for e in range(experts):
        zr = jnp.sum(jnp.where(zrow == core * experts + e, z_own, 0.0), axis=0, keepdims=True)
        z_inv.append(1.0 / jnp.sum(jnp.where(eye, zr, 0.0), axis=1, keepdims=True))

    _drain(wi_v, wi_sem)
    for k, off, wd in chunks:
        _drain(q_in[k].at[pl.ds(0, 7)], qr_sem.at[k])
        for cs in range(2):
            for q in range(GROUPS):
                p = cs * GROUPS + q
                s = [q_in[k][4 * cs + j, q // 2, q % 2].astype(F32) for j in range(4)]
                s = (s[0] + s[1]) + (s[2] + s[3])
                for t in range(wd // 128):
                    xs_f[t, p * chip_rows:(p + 1) * chip_rows, :] = s[:, t * 128:(t + 1) * 128]
        for e in range(experts):
            pick = pl.ds(e, rows, stride=experts)
            xe = [(xs_f[t, pick, :] * z_inv[e]).astype(BF16) for t in range(wd // 128)]
            xe = xe[0] if len(xe) == 1 else jnp.concatenate(xe, axis=1)
            h = _nn(xe, wi_v[e, off:off + wd, :])
            hid[e] = h if k == 0 else hid[e] + h
    _drain(wo_v, wo_sem)
    for e in range(experts):
        hid_b[e] = jax.nn.gelu(hid[e], approximate=True).astype(BF16)

    def y_copy(k, h, f):
        dc = dst_at(h, f)[0]
        return pltpu.make_async_remote_copy(
            yx[k].at[dc * 2 + h], g_in[k].at[src_at(h), h],
            ys_sem, yr_sem.at[k], device_id=group_peer(2 * h, f), device_id_type=MESH)

    def g_copy(k, q, s):
        ref = gath[k].at[(pl.ds(own0 + q * gsz, gsz),) + region(ORDERS[q], s + 1)]
        return pltpu.make_async_remote_copy(
            ref, ref, gs_sem.at[s], gr_sem.at[2 * k + s], device_id=steps[ORDERS[q][s]], device_id_type=MESH)

    def gd_copy(k):
        at = pl.ds(own0, hrows)
        return pltpu.make_async_remote_copy(
            gath[k].at[at], g_hbm[k].at[at], gds_sem, gdr_sem, device_id=mate, device_id_type=MESH)

    def go_copy(k):
        at = pl.ds(own0, hrows)
        return pltpu.make_async_copy(gath[k].at[at], g_hbm[k].at[at], go_sem)

    for base in range(0, width, WIDE):
        for e in range(experts):
            ye = _nn(hid_b[e], wo_v[e, :, base:base + WIDE])
            for t in range(WIDE // 128):
                ys_f[t, pl.ds(e, rows, stride=experts), :] = ye[:, t * 128:(t + 1) * 128]
        for k, off, wd in chunks:
            if not base <= off < base + WIDE:
                continue
            for t in range(wd // 128):
                rows8 = ys_f[t + (off - base) // 128].reshape(4, 2, chip_rows, 128)
                yx[k][:, :, :, t * 128:(t + 1) * 128] = rows8.astype(BF16)
            for h in range(2):
                for f in range(7):
                    y_copy(k, h, f).start()
                g_in[k][src_at(h), h] = yx[k][core * 2 + h]

    for k, _, wd in chunks:
        _drain(g_in[k].at[pl.ds(0, 7)], yr_sem.at[k])
        for q in range(GROUPS):
            for u in range(2):
                for v in range(2):
                    s0 = g_in[k][2 * u + v, q // 2, q % 2].astype(F32)
                    s1 = g_in[k][4 + 2 * u + v, q // 2, q % 2].astype(F32)
                    at = at_rest(q, u, v)
                    b = own0 + q * gsz
                    gath[k][(b,) + at] = jnp.where(low(wd), s0, pltpu.roll(s1, experts, 0)).astype(BF16)
                    gath[k][(b + 1,) + at] = jnp.where(low(wd), pltpu.roll(s0, experts, 0), s1).astype(BF16)
        for q in range(GROUPS):
            g_copy(k, q, 1).start()
    for k in range(NK):
        _drain(r1[k], gr_sem.at[2 * k + 1])
        for q in range(GROUPS):
            g_copy(k, q, 0).start()
    for k in range(NK):
        _drain(r0[k], gr_sem.at[2 * k])
        gd_copy(k).start()
        go_copy(k).start()
    c_copy.wait()
    zh_bytes = x_v.at[pl.ds(0, hrows)]
    r0_bytes = x_v.at[pl.ds(0, hrows // 2)]
    r1_bytes = x_v.at[pl.ds(0, hrows // 4)]
    q_bytes = x_v.at[pl.ds(0, 7), pl.ds(0, 32)]
    z_copy(0).wait_send()
    z_copy(1).wait_send()
    _drain(zq, zs_sem.at[2])
    _drain(zh_bytes, hs_sem)
    _drain(r0_bytes, rs_sem.at[0])
    _drain(r1_bytes, rs_sem.at[1])
    _drain(q_bytes, qs_sem)
    _drain(q_bytes, ys_sem)
    _drain(r0_bytes, gs_sem.at[0])
    _drain(r1_bytes, gs_sem.at[1])
    _drain(zh_bytes, gds_sem)
    _drain(zh_bytes, go_sem)
    _drain(zh_bytes, gdr_sem)


def _mix_kernel(*refs):
    len_ref = refs[0]
    g_hbm = refs[1:1 + NK]
    c_hbm, y_hbm, g_v, c_v, y_v, g_sem, c_sem, y_sem = refs[1 + NK:]
    rows, tok_count, width = y_v.shape
    step = rows // 4

    def c_copy(b):
        at = pl.ds(b, step)
        return pltpu.make_async_copy(c_hbm.at[at], c_v.at[at], c_sem.at[b // step])

    def g_copies(b):
        at = pl.ds(b, step)
        return [
            pltpu.make_async_copy(
                g_hbm[k].at[at], g_v.at[at, :, pl.ds(OFFS[k], WIDTHS[k])], g_sem.at[b // step])
            for k in range(NK)
        ]

    def y_copy(b):
        at = pl.ds(b, step)
        return pltpu.make_async_copy(y_v.at[at], y_hbm.at[at], y_sem)

    for b in range(0, rows, step):
        c_copy(b).start()
        for cp in g_copies(b):
            cp.start()
    row_pos = lax.axis_index("seq") * tok_count + lax.broadcasted_iota(jnp.int32, (tok_count, WIDE), 0)
    for b0 in range(0, rows, step):
        c_copy(b0).wait()
        _drain(g_v.at[pl.ds(b0, step)], g_sem.at[b0 // step])
        for b in range(b0, b0 + step):
            for off in range(0, width, WIDE):
                yk = jnp.where(row_pos < len_ref[b], _nn(c_v[b], g_v[b, :, off:off + WIDE]), 0.0)
                y_v[b, :, off:off + WIDE] = yk.astype(BF16)
        y_copy(b0).start()
    _drain(y_v, y_sem)


def solution(mesh):
    def shard_body(tok, lens, phi, gain, w_in, w_out):
        rows, tok_count, width = tok.shape
        experts, _, ff = w_in.shape
        nslots = phi.shape[1]
        hrows = rows // 2
        cr = 2 * experts
        cube = (2, 2, 2, 2)
        lanes = WIDE // 128
        vm = pltpu.VMEM
        dma = pltpu.SemaphoreType.DMA
        anyspace = pl.BlockSpec(memory_space=pl.ANY)
        smem = pl.BlockSpec(memory_space=pltpu.SMEM)

        def per_chunk(*lead):
            return [vm(lead + (cr, wd), BF16) for wd in WIDTHS]

        scratch = [
            vm((rows, tok_count, width), BF16),
            vm((rows, tok_count, width), BF16),
            vm((rows, nslots, tok_count), BF16),
            vm((width, nslots), BF16),
            vm((nslots, width), BF16),
            vm(w_in.shape, BF16),
            vm(w_out.shape, BF16),
            vm((rows, nslots, tok_count), BF16),
            vm((rows, tok_count, nslots), BF16),
            *per_chunk(rows, *cube),
            *per_chunk(hrows, *cube),
            *per_chunk(hrows, 2, 2, 2),
            *per_chunk(hrows, 2, 2),
            *per_chunk(2, 8, 2),
            *per_chunk(8, 2, 2),
            *per_chunk(4, 2),
            *per_chunk(8, 2, 2),
            *per_chunk(rows, *cube),
            vm(cube + (cr, tok_count), F32),
            vm(cube + (cr, tok_count), F32),
            vm((2, 2, 2, cr, tok_count), F32),
            vm((2, 2, cr, tok_count), F32),
            vm((3, cr, tok_count), F32),
            vm((lanes, rows * experts, 128), F32),
            vm((experts, rows, ff), F32),
            vm((experts, rows, ff), BF16),
            vm((lanes, rows * experts, 128), F32),
            dma, dma((4,)), dma, dma, dma, dma, dma((NK,)), dma, dma, dma((3,)), dma((3,)),
            dma((2,)), dma((2 * NK,)), dma, dma((NK,)), dma, dma((NK,)), dma((2,)), dma((2 * NK,)), dma, dma, dma,
        ]
        gshapes = [jax.ShapeDtypeStruct((rows,) + cube + (cr, wd), BF16) for wd in WIDTHS]
        *gath, comb = pl.pallas_call(
            _exchange_kernel,
            out_shape=(*gshapes, jax.ShapeDtypeStruct((rows, tok_count, nslots), BF16)),
            in_specs=[smem, smem, anyspace, anyspace, anyspace, anyspace],
            out_specs=(anyspace,) * (NK + 1),
            scratch_shapes=scratch,
            compiler_params=pltpu.CompilerParams(
                collective_id=0, has_side_effects=True, vmem_limit_bytes=67043328),
        )(lens, gain, tok, phi, w_in, w_out)
        return pl.pallas_call(
            _mix_kernel,
            out_shape=jax.ShapeDtypeStruct(tok.shape, BF16),
            in_specs=[smem] + [anyspace] * (NK + 1),
            out_specs=anyspace,
            scratch_shapes=[
                vm((rows, nslots, width), BF16),
                vm((rows, tok_count, nslots), BF16),
                vm(tok.shape, BF16),
                dma((4,)), dma((4,)), dma,
            ],
        )(lens, *[g.reshape(rows, nslots, wd) for g, wd in zip(gath, WIDTHS)], comb)

    return jax.shard_map(
        shard_body,
        mesh=mesh,
        in_specs=(P("data", "seq", None), P("data"), P(None, None), P(None), P("seq", None, None), P("seq", None, None)),
        out_specs=P("data", "seq", None),
        check_vma=False,
    )
```

time: 53.2 us -> 51.4 us (0.966)
  Pallas kernels: 52.3 us -> 50.5 us
    pallas_call x1, Pallas kernels: 47.5 us -> 45.8 us  [shard_body(): pl.pallas_call(_exchange_kernel, out_shape=(*gshapes, jax.ShapeDtypeStruc...]
where the time goes in v5:
time: 51.4 us; the launch traced here: 51.3 us
  Pallas kernels  50.5 us (98%)
  between operations  0.82 us (2%)
    pallas_call x1, Pallas kernels, shard_body(): pl.pallas_call(_exchange_kernel, out_shape=(*gshapes, jax.ShapeDtypeStruc...  45.8 us
    pallas_call x1, Pallas kernels, shard_body(): pl.pallas_call(_mix_kernel, out_shape=jax.ShapeDtypeStruct(tok.shape, BF1...  4.66 us

profile of v5, /device:TPU:97, one launch (start us, length us, event | category | flops | bytes accessed | tf_op | source)
XLA Modules:
  0.0 51.3 jit_solution(12935121669241418946)
XLA Ops:
  0.7 45.8 %shard_map.64 = (bf16[16,2,2,2,2,8,256]{6,5,4,3,2,1,0:T(8,128)(2,1)}, bf16[16,2,2,2,2,8,256]{6,5,4,3,2,1,0:T(8,128)(2,1)}, bf16[16,2,2,2,2,8,128]{6,5,4,3,2,1,0:...) custom-call(s32[16]{0:T(128)} %refs_0_.3, f32[1]{0:T(128)S(6)} %copy.7.refs_1_, ...), custom_call_target="tpu_custom_call" | custom-call | tf_op jit(solution)/shard_map/pallas_call | solution.py:506
  46.5 4.7 %shard_map.65 = bf16[16,128,768]{2,1,0:T(8,128)(2,1)} custom-call(s32[16]{0:T(128)} %refs_0_.3, bf16[16,128,256]{2,1,0:T(8,128)(2,1)} %bitcast.4, bf16[16,128,256]{2,1,0:T(8,128)(2,1)} %bitcast.5, bf16[16,128,128]{2,1,0:T(8,128)(2,1)} %bitcast.6, bf16[16,128,128]{2,1,0:T(8,128)(2,1)} %bitcast.7, bf16[16,128,128]{2,1,0:T(8,128)(2,1)} %get-tuple-element.14.refs_5_), custom_call_target="tpu_custom_call" | custom-call | tf_op jit(solution)/shard_map/pallas_call | solution.py:515

commit v6 on v5

--- a/solution.py
+++ b/solution.py
@@ -154,7 +154,7 @@
         return pltpu.make_async_remote_copy(
             part[k].at[(pl.ds(own0 + q * gsz, gsz),) + region(order, s, order[s])],
             rbuf[s][k].at[pl.ds(q * gsz, gsz)],
-            rs_sem.at[s], rr_sem.at[2 * k + s], device_id=steps[order[s]], device_id_type=MESH)
+            rs_sem.at[k if s == 0 else NK], rr_sem.at[2 * k + s], device_id=steps[order[s]], device_id_type=MESH)
 
     def z_copy(s):
         order = ORDERS[0]
@@ -218,26 +218,29 @@
     front(2 * tok_step, rows, range(3 * tok_step, rows))
     zh_copy.start()
 
-    for k in range(NK):
+    def halve(k):
         _drain(half_in[k], hr_sem.at[k])
         for j in range(hrows):
             part[k][own0 + j] = part[k][own0 + j] + half_in[k][j]
         for q in range(GROUPS):
             rs_copy(k, q, 0).start()
 
-    zh_copy.wait()
-    z_part[...] += z_half[...]
-    z_copy(0).start()
-
-
     def flip_c(i, carry):
         for u in range(4):
             c_v[4 * i + u] = ct_v[4 * i + u].astype(F32).T.astype(BF16)
         return carry
 
+    halve(0)
     lax.fori_loop(0, rows // 4, flip_c, 0)
     c_copy = pltpu.make_async_copy(c_v, c_hbm, c_sem)
     c_copy.start()
+    halve(1)
+    zh_copy.wait()
+    z_part[...] += z_half[...]
+    z_copy(0).start()
+    _drain(r0[0], rs_sem.at[0])
+    for k in range(2, NK):
+        halve(k)
 
     def src_at(h):
         o = ORDERS[2 * h]
@@ -319,6 +322,7 @@
         z_inv.append(1.0 / jnp.sum(jnp.where(eye, zr, 0.0), axis=1, keepdims=True))
 
     _drain(wi_v, wi_sem)
+    _drain(wo_v, wo_sem)
     for k, off, wd in chunks:
         _drain(q_in[k].at[pl.ds(0, 7)], qr_sem.at[k])
         for cs in range(2):
@@ -334,7 +338,6 @@
             xe = xe[0] if len(xe) == 1 else jnp.concatenate(xe, axis=1)
             h = _nn(xe, wi_v[e, off:off + wd, :])
             hid[e] = h if k == 0 else hid[e] + h
-    _drain(wo_v, wo_sem)
     for e in range(experts):
         hid_b[e] = jax.nn.gelu(hid[e], approximate=True).astype(BF16)
 
@@ -404,8 +407,9 @@
     z_copy(1).wait_send()
     _drain(zq, zs_sem.at[2])
     _drain(zh_bytes, hs_sem)
-    _drain(r0_bytes, rs_sem.at[0])
-    _drain(r1_bytes, rs_sem.at[1])
+    for k in range(1, NK):
+        _drain(r0[k], rs_sem.at[k])
+    _drain(r1_bytes, rs_sem.at[NK])
     _drain(q_bytes, qs_sem)
     _drain(q_bytes, ys_sem)
     _drain(r0_bytes, gs_sem.at[0])
@@ -500,7 +504,7 @@
             vm((experts, rows, ff), BF16),
             vm((lanes, rows * experts, 128), F32),
             dma, dma((4,)), dma, dma, dma, dma, dma((NK,)), dma, dma, dma((3,)), dma((3,)),
-            dma((2,)), dma((2 * NK,)), dma, dma((NK,)), dma, dma((NK,)), dma((2,)), dma((2 * NK,)), dma, dma, dma,
+            dma((NK + 1,)), dma((2 * NK,)), dma, dma((NK,)), dma, dma((NK,)), dma((2,)), dma((2 * NK,)), dma, dma, dma,
         ]
         gshapes = [jax.ShapeDtypeStruct((rows,) + cube + (cr, wd), BF16) for wd in WIDTHS]
         *gath, comb = pl.pallas_call(

time: 51.4 us -> 50.7 us (0.986)
  Pallas kernels: 50.5 us -> 49.8 us
    pallas_call x1, Pallas kernels: 45.8 us -> 45.1 us  [shard_body(): pl.pallas_call(_exchange_kernel, out_shape=(*gshapes, jax.ShapeDtypeStruc...]
where the time goes in v6:
time: 50.7 us; the launch traced here: 50.6 us
  Pallas kernels  49.8 us (98%)
  between operations  0.82 us (2%)
    pallas_call x1, Pallas kernels, shard_body(): pl.pallas_call(_exchange_kernel, out_shape=(*gshapes, jax.ShapeDtypeStruc...  45.1 us
    pallas_call x1, Pallas kernels, shard_body(): pl.pallas_call(_mix_kernel, out_shape=jax.ShapeDtypeStruct(tok.shape, BF1...  4.66 us

profile of v6, /device:TPU:97, one launch (start us, length us, event | category | flops | bytes accessed | tf_op | source)
XLA Modules:
  0.0 50.6 jit_solution(4765726702424205193)
XLA Ops:
  0.7 45.1 %shard_map.64 = (bf16[16,2,2,2,2,8,256]{6,5,4,3,2,1,0:T(8,128)(2,1)}, bf16[16,2,2,2,2,8,256]{6,5,4,3,2,1,0:T(8,128)(2,1)}, bf16[16,2,2,2,2,8,128]{6,5,4,3,2,1,0:...) custom-call(s32[16]{0:T(128)} %refs_0_.3, f32[1]{0:T(128)S(6)} %copy.7.refs_1_, ...), custom_call_target="tpu_custom_call" | custom-call | tf_op jit(solution)/shard_map/pallas_call | solution.py:510
  45.8 4.7 %shard_map.65 = bf16[16,128,768]{2,1,0:T(8,128)(2,1)} custom-call(s32[16]{0:T(128)} %refs_0_.3, bf16[16,128,256]{2,1,0:T(8,128)(2,1)} %bitcast.4, bf16[16,128,256]{2,1,0:T(8,128)(2,1)} %bitcast.5, bf16[16,128,128]{2,1,0:T(8,128)(2,1)} %bitcast.6, bf16[16,128,128]{2,1,0:T(8,128)(2,1)} %bitcast.7, bf16[16,128,128]{2,1,0:T(8,128)(2,1)} %get-tuple-element.14.refs_5_), custom_call_target="tpu_custom_call" | custom-call | tf_op jit(solution)/shard_map/pallas_call | solution.py:519

commit v7 on v6

--- a/solution.py
+++ b/solution.py
@@ -44,12 +44,12 @@
     part, half_in, r0, r1, q_out, q_in, yx, g_in, gath = [take() for _ in range(9)]
     z_part, z_half, z0, z1, zq, xs_f, hid, hid_b, ys_f = take(9)
     (phi_sem, tok_sem, wi_sem, wo_sem, c_sem, hs_sem, hr_sem, zhs_sem, zhr_sem, zs_sem, zr_sem,
-     rs_sem, rr_sem, qs_sem, qr_sem, ys_sem, yr_sem, gs_sem, gr_sem, gds_sem, gdr_sem, go_sem) = take(22)
+     rs_sem, rr_sem, qs_sem, qr_sem, ys_sem, yr_sem, gs_sem, gr_sem, gds_sem, gdr_sem, go_sem, fl_sem, fs_sem, fr_sem) = take(25)
     rows, tok_count, width = x_v.shape
     experts = wi_v.shape[0]
     hrows = rows // 2
     gsz = hrows // GROUPS
-    nslots = phit_v.shape[0]
+    nslots = phit_v.shape[1]
     chip_rows = 2 * experts
     chunks = tuple(zip(range(NK), OFFS, WIDTHS))
     me = lax.axis_index("seq")
@@ -116,7 +116,7 @@
 
     def weigh(i):
         b = batch(i)
-        ex = jnp.exp(_nt(phit_v[...], xn_v[i]) - shift)
+        ex = jnp.exp(_nt(phit_v[i % 2], xn_v[i]) - shift)
         ct_v[b] = (ex * (1.0 / jnp.sum(ex, axis=0, keepdims=True))).astype(BF16)
         exm = jnp.where(pos < len_ref[b], ex, 0.0)
         w_v[i] = exm.astype(BF16)
@@ -189,8 +189,9 @@
     nchip = new // chip_rows
     nxa, nxb, nya, nyb = nchip & 1, (nchip >> 1) & 1, (nchip >> 2) & 1, (nchip >> 3) & 1
     src = ((2 * nyb + (nya ^ nyb)) * 4 + 2 * nxb + (nxa ^ nxb)) * chip_rows + (new & (chip_rows - 1))
-    perm = jnp.where(src == old, 1.0, 0.0).astype(BF16)
-    phit_v[...] = _nt(perm, pn).astype(BF16)
+    for odd in range(2):
+        perm = jnp.where((src ^ (odd * experts)) == old, 1.0, 0.0).astype(BF16)
+        phit_v[odd] = _nt(perm, pn).astype(BF16)
     for cp in wi_copies + wo_copies:
         cp.start()
 
@@ -299,8 +300,8 @@
                         for w in range(gsz)
                     ]
                     d = 2 * u + v
-                    q_out[k][h, d, g] = jnp.where(low(wd), ev, pltpu.roll(od, experts, 0)).astype(BF16)
-                    q_out[k][h, 4 + d, g] = jnp.where(low(wd), pltpu.roll(ev, experts, 0), od).astype(BF16)
+                    q_out[k][h, d, g] = jnp.where(low(wd), ev, od).astype(BF16)
+                    q_out[k][h, 4 + d, g] = jnp.where(low(wd), od, ev).astype(BF16)
         for h in range(2):
             for f in range(7):
                 q_copy(k, h, f).start()
@@ -314,11 +315,13 @@
     _drain(zq, zr_sem.at[2])
     z_own = z_part[bits] + (zq[0] + (zq[1] + zq[2]))
     zrow = lax.broadcasted_iota(jnp.int32, z_own.shape, 0)
-    eye = lax.broadcasted_iota(jnp.int32, (rows, z_own.shape[1]), 0) == lax.broadcasted_iota(
-        jnp.int32, (rows, z_own.shape[1]), 1)
+    zcol = lax.broadcasted_iota(jnp.int32, z_own.shape, 1)
+    zbase = (core ^ (zcol & 1)) * experts
+    erow = lax.broadcasted_iota(jnp.int32, (rows, z_own.shape[1]), 0)
+    eye = (erow ^ core) == lax.broadcasted_iota(jnp.int32, (rows, z_own.shape[1]), 1)
     z_inv = []
     for e in range(experts):
-        zr = jnp.sum(jnp.where(zrow == core * experts + e, z_own, 0.0), axis=0, keepdims=True)
+        zr = jnp.sum(jnp.where(zrow == zbase + e, z_own, 0.0), axis=0, keepdims=True)
         z_inv.append(1.0 / jnp.sum(jnp.where(eye, zr, 0.0), axis=1, keepdims=True))
 
     _drain(wi_v, wi_sem)
@@ -357,6 +360,16 @@
         return pltpu.make_async_remote_copy(
             gath[k].at[at], g_hbm[k].at[at], gds_sem, gdr_sem, device_id=mate, device_id_type=MESH)
 
+    def last_copies(q):
+        dim = ORDERS[q][0]
+        at = (pl.ds(own0 + q * gsz, gsz),) + region(ORDERS[q], 1)
+        src, dst = gath[NK - 1].at[at], g_hbm[NK - 1].at[at]
+        return [pltpu.make_async_copy(src, dst, fl_sem)] + [
+            pltpu.make_async_remote_copy(
+                src, dst, fs_sem.at[t], fr_sem.at[t], device_id=d, device_id_type=MESH)
+            for t, d in enumerate((peer((dim,), 1), steps[dim], mate))
+        ]
+
     def go_copy(k):
         at = pl.ds(own0, hrows)
         return pltpu.make_async_copy(gath[k].at[at], g_hbm[k].at[at], go_sem)
@@ -386,15 +399,24 @@
                     s1 = g_in[k][4 + 2 * u + v, q // 2, q % 2].astype(F32)
                     at = at_rest(q, u, v)
                     b = own0 + q * gsz
-                    gath[k][(b,) + at] = jnp.where(low(wd), s0, pltpu.roll(s1, experts, 0)).astype(BF16)
-                    gath[k][(b + 1,) + at] = jnp.where(low(wd), pltpu.roll(s0, experts, 0), s1).astype(BF16)
+                    gath[k][(b,) + at] = jnp.where(low(wd), s0, s1).astype(BF16)
+                    gath[k][(b + 1,) + at] = jnp.where(low(wd), s1, s0).astype(BF16)
         for q in range(GROUPS):
             g_copy(k, q, 1).start()
     for k in range(NK):
         _drain(r1[k], gr_sem.at[2 * k + 1])
+
+        @pl.when(core == 1)
+        def _():
+            pl.delay((300, 350, 550, 600)[k])
+
         for q in range(GROUPS):
-            g_copy(k, q, 0).start()
-    for k in range(NK):
+            if k < NK - 1:
+                g_copy(k, q, 0).start()
+            else:
+                for cp in last_copies(q):
+                    cp.start()
+    for k in range(NK - 1):
         _drain(r0[k], gr_sem.at[2 * k])
         gd_copy(k).start()
         go_copy(k).start()
@@ -412,11 +434,17 @@
     _drain(r1_bytes, rs_sem.at[NK])
     _drain(q_bytes, qs_sem)
     _drain(q_bytes, ys_sem)
-    _drain(r0_bytes, gs_sem.at[0])
+    most = pl.ds(0, width - WIDTHS[-1])
+    g_bytes = x_v.at[pl.ds(0, hrows), :, most]
+    _drain(x_v.at[pl.ds(0, hrows // 2), :, most], gs_sem.at[0])
     _drain(r1_bytes, gs_sem.at[1])
-    _drain(zh_bytes, gds_sem)
-    _drain(zh_bytes, go_sem)
-    _drain(zh_bytes, gdr_sem)
+    _drain(g_bytes, gds_sem)
+    _drain(g_bytes, go_sem)
+    _drain(g_bytes, gdr_sem)
+    _drain(r0[NK - 1], fl_sem)
+    for t in range(3):
+        _drain(r0[NK - 1], fs_sem.at[t])
+        _drain(r0[NK - 1], fr_sem.at[t])
 
 
 def _mix_kernel(*refs):
@@ -443,6 +471,8 @@
         return pltpu.make_async_copy(y_v.at[at], y_hbm.at[at], y_sem)
 
     for b in range(0, rows, step):
+        if b:
+            pl.delay(250)
         c_copy(b).start()
         for cp in g_copies(b):
             cp.start()
@@ -480,7 +510,7 @@
             vm((rows, tok_count, width), BF16),
             vm((rows, nslots, tok_count), BF16),
             vm((width, nslots), BF16),
-            vm((nslots, width), BF16),
+            vm((2, nslots, width), BF16),
             vm(w_in.shape, BF16),
             vm(w_out.shape, BF16),
             vm((rows, nslots, tok_count), BF16),
@@ -505,6 +535,7 @@
             vm((lanes, rows * experts, 128), F32),
             dma, dma((4,)), dma, dma, dma, dma, dma((NK,)), dma, dma, dma((3,)), dma((3,)),
             dma((NK + 1,)), dma((2 * NK,)), dma, dma((NK,)), dma, dma((NK,)), dma((2,)), dma((2 * NK,)), dma, dma, dma,
+            dma, dma((3,)), dma((3,)),
         ]
         gshapes = [jax.ShapeDtypeStruct((rows,) + cube + (cr, wd), BF16) for wd in WIDTHS]
         *gath, comb = pl.pallas_call(

time: 50.7 us -> 50 us (0.986)
  Pallas kernels: 49.8 us -> 49.2 us
where the time goes in v7:
time: 50 us; the launch traced here: 49.9 us
  Pallas kernels  49.2 us (98%)
  between operations  0.66 us (1%)
    pallas_call x1, Pallas kernels, shard_body(): pl.pallas_call(_exchange_kernel, out_shape=(*gshapes, jax.ShapeDtypeStruc...  45 us
    pallas_call x1, Pallas kernels, shard_body(): pl.pallas_call(_mix_kernel, out_shape=jax.ShapeDtypeStruct(tok.shape, BF1...  4.19 us

profile of v7, /device:TPU:97, one launch (start us, length us, event | category | flops | bytes accessed | tf_op | source)
XLA Modules:
  0.0 49.9 jit_solution(15715353362873285496)
XLA Ops:
  0.7 45.0 %shard_map.64 = (bf16[16,2,2,2,2,8,256]{6,5,4,3,2,1,0:T(8,128)(2,1)}, bf16[16,2,2,2,2,8,256]{6,5,4,3,2,1,0:T(8,128)(2,1)}, bf16[16,2,2,2,2,8,128]{6,5,4,3,2,1,0:...) custom-call(s32[16]{0:T(128)} %refs_0_.3, f32[1]{0:T(128)S(6)} %copy.7.refs_1_, ...), custom_call_target="tpu_custom_call" | custom-call | tf_op jit(solution)/shard_map/pallas_call | solution.py:541
  45.7 4.2 %shard_map.65 = bf16[16,128,768]{2,1,0:T(8,128)(2,1)} custom-call(s32[16]{0:T(128)} %refs_0_.3, bf16[16,128,256]{2,1,0:T(8,128)(2,1)} %bitcast.4, bf16[16,128,256]{2,1,0:T(8,128)(2,1)} %bitcast.5, bf16[16,128,128]{2,1,0:T(8,128)(2,1)} %bitcast.6, bf16[16,128,128]{2,1,0:T(8,128)(2,1)} %bitcast.7, bf16[16,128,128]{2,1,0:T(8,128)(2,1)} %get-tuple-element.14.refs_5_), custom_call_target="tpu_custom_call" | custom-call | tf_op jit(solution)/shard_map/pallas_call | solution.py:550

commit v8 on v7

--- a/solution.py
+++ b/solution.py
@@ -223,6 +223,11 @@
         _drain(half_in[k], hr_sem.at[k])
         for j in range(hrows):
             part[k][own0 + j] = part[k][own0 + j] + half_in[k][j]
+
+        @pl.when(core == 1)
+        def _():
+            pl.delay(250)
+
         for q in range(GROUPS):
             rs_copy(k, q, 0).start()
 
@@ -401,6 +406,11 @@
                     b = own0 + q * gsz
                     gath[k][(b,) + at] = jnp.where(low(wd), s0, s1).astype(BF16)
                     gath[k][(b + 1,) + at] = jnp.where(low(wd), s1, s0).astype(BF16)
+
+        @pl.when(core == 1)
+        def _():
+            pl.delay(200)
+
         for q in range(GROUPS):
             g_copy(k, q, 1).start()
     for k in range(NK):

time: 50 us -> 49.7 us (level)
  no operation moved by 1% of the time
where the time goes in v8:
time: 49.7 us; the launch traced here: 49.6 us
  Pallas kernels  48.9 us (98%)
  between operations  0.66 us (1%)
    pallas_call x1, Pallas kernels, shard_body(): pl.pallas_call(_exchange_kernel, out_shape=(*gshapes, jax.ShapeDtypeStruc...  44.7 us
    pallas_call x1, Pallas kernels, shard_body(): pl.pallas_call(_mix_kernel, out_shape=jax.ShapeDtypeStruct(tok.shape, BF1...  4.19 us

profile of v8, /device:TPU:97, one launch (start us, length us, event | category | flops | bytes accessed | tf_op | source)
XLA Modules:
  0.0 49.6 jit_solution(17084723778728212475)
XLA Ops:
  0.7 44.7 %shard_map.64 = (bf16[16,2,2,2,2,8,256]{6,5,4,3,2,1,0:T(8,128)(2,1)}, bf16[16,2,2,2,2,8,256]{6,5,4,3,2,1,0:T(8,128)(2,1)}, bf16[16,2,2,2,2,8,128]{6,5,4,3,2,1,0:...) custom-call(s32[16]{0:T(128)} %refs_0_.3, f32[1]{0:T(128)S(6)} %copy.7.refs_1_, ...), custom_call_target="tpu_custom_call" | custom-call | tf_op jit(solution)/shard_map/pallas_call | solution.py:551
  45.4 4.2 %shard_map.65 = bf16[16,128,768]{2,1,0:T(8,128)(2,1)} custom-call(s32[16]{0:T(128)} %refs_0_.3, bf16[16,128,256]{2,1,0:T(8,128)(2,1)} %bitcast.4, bf16[16,128,256]{2,1,0:T(8,128)(2,1)} %bitcast.5, bf16[16,128,128]{2,1,0:T(8,128)(2,1)} %bitcast.6, bf16[16,128,128]{2,1,0:T(8,128)(2,1)} %bitcast.7, bf16[16,128,128]{2,1,0:T(8,128)(2,1)} %get-tuple-element.14.refs_5_), custom_call_target="tpu_custom_call" | custom-call | tf_op jit(solution)/shard_map/pallas_call | solution.py:560

commit v9 on v8

--- a/solution.py
+++ b/solution.py
@@ -409,7 +409,7 @@
 
         @pl.when(core == 1)
         def _():
-            pl.delay(200)
+            pl.delay(350)
 
         for q in range(GROUPS):
             g_copy(k, q, 1).start()

time: 49.7 us -> 49.7 us (level)
  no operation moved by 1% of the time
where the time goes in v9:
time: 49.7 us; the launch traced here: 49.6 us
  Pallas kernels  48.9 us (98%)
  between operations  0.66 us (1%)
    pallas_call x1, Pallas kernels, shard_body(): pl.pallas_call(_exchange_kernel, out_shape=(*gshapes, jax.ShapeDtypeStruc...  44.7 us
    pallas_call x1, Pallas kernels, shard_body(): pl.pallas_call(_mix_kernel, out_shape=jax.ShapeDtypeStruct(tok.shape, BF1...  4.19 us

profile of v9, /device:TPU:97, one launch (start us, length us, event | category | flops | bytes accessed | tf_op | source)
XLA Modules:
  0.0 49.6 jit_solution(7491357289824677827)
XLA Ops:
  0.7 44.7 %shard_map.64 = (bf16[16,2,2,2,2,8,256]{6,5,4,3,2,1,0:T(8,128)(2,1)}, bf16[16,2,2,2,2,8,256]{6,5,4,3,2,1,0:T(8,128)(2,1)}, bf16[16,2,2,2,2,8,128]{6,5,4,3,2,1,0:...) custom-call(s32[16]{0:T(128)} %refs_0_.3, f32[1]{0:T(128)S(6)} %copy.7.refs_1_, ...), custom_call_target="tpu_custom_call" | custom-call | tf_op jit(solution)/shard_map/pallas_call | solution.py:551
  45.4 4.2 %shard_map.65 = bf16[16,128,768]{2,1,0:T(8,128)(2,1)} custom-call(s32[16]{0:T(128)} %refs_0_.3, bf16[16,128,256]{2,1,0:T(8,128)(2,1)} %bitcast.4, bf16[16,128,256]{2,1,0:T(8,128)(2,1)} %bitcast.5, bf16[16,128,128]{2,1,0:T(8,128)(2,1)} %bitcast.6, bf16[16,128,128]{2,1,0:T(8,128)(2,1)} %bitcast.7, bf16[16,128,128]{2,1,0:T(8,128)(2,1)} %get-tuple-element.14.refs_5_), custom_call_target="tpu_custom_call" | custom-call | tf_op jit(solution)/shard_map/pallas_call | solution.py:560
